TPU v7x, 256 devices: a whole 4x4x8 slice. The times are simulated.
256 devices in a mesh: dp: 32 (over y, x, core), section: 8 (over z).
Axes of the slice: x: 4, y: 4, z: 8, core: 2. Of those that a mesh axis runs over, the one named last changes fastest.
Arguments:
- activations: bfloat16 [4, 2048, 2048], P(None, 'dp'), may hold values from -6 to 6
- cotangent: bfloat16 [4, 2048, 2048], P(None, 'dp'), may hold values from -6 to 6
- weight: bfloat16 [8, 2048, 2048], P('section', 'dp'), may hold values from -0.125 to 0.125
- norm_gain: float32 [8, 2048], P('section'), may hold values from 0.1 to 1.9
- pair_mask: int32 [8, 512, 2048], P('section'), may hold values from 0 to 5, as said below
- earlier_mask: int32 [8, 512, 2048], P('section', 'dp'), may hold values from 0 to 5, as said below
Outputs:
- weight_grad: float32 [8, 2048, 2048], P('section', 'dp')
- flip_count: int32 [8], P('section')
Inputs may be any that keep to these rules, and one draw needn't show every extreme that they name: `pair_mask`: pair number of each group of four consecutive rows and each column; pairs numbered (0,1), (0,2), (0,3), (1,2), (1,3), (2,3). `earlier_mask`: pair numbers of the previous step, numbered likewise.
All inputs are finite; a program needn't handle non-finite values.
Results may differ from a plain program's by a relative error of at most 0.02.
Values may be sent and summed in bfloat16 or wider, within the bound.
A program may use at most 64 MiB of HBM per device.

v0:
```python
import math

import jax
import jax.numpy as jnp
from jax import lax
from jax.sharding import PartitionSpec as P

epsilon = 1e-06
decay_rate = 4.0
half_root = 0.7071067811865476
density_scale = 0.3989422804014327
first_table = (0, 0, 0, 1, 1, 2)
second_table = (1, 2, 3, 2, 3, 3)


def copy_for_each(x, axis):
    copies = jnp.broadcast_to(x, (lax.axis_size(axis), *x.shape))
    return lax.all_to_all(copies, axis, split_axis=0, concat_axis=0, tiled=True)


def of_everyone(x, axis):
    return copy_for_each(x, axis).sum(axis=0)


def shifted(block, axis, distance):
    devices = range(lax.axis_size(axis))
    route = [(i - distance, i) for i in devices if i - distance in devices]
    return lax.ppermute(block, axis, route)


def pair_ends(indices):
    leading = jnp.zeros_like(indices)
    trailing = jnp.zeros_like(indices)
    for pair_index in range(6):
        matches = indices == pair_index
        leading = jnp.where(matches, first_table[pair_index], leading)
        trailing = jnp.where(matches, second_table[pair_index], trailing)
    return (leading, trailing)


def kept_positions(indices):
    leading, trailing = pair_ends(indices)
    groups, columns = indices.shape
    positions = lax.broadcasted_iota(jnp.int32, (groups, 4, columns), 1)
    kept_mask = (positions == leading[:, None, :]) | (positions == trailing[:, None, :])
    return kept_mask.reshape(groups * 4, columns)


def section_forward(inputs, masked, gain_row):
    values = inputs.astype(jnp.float32)
    norm_scale = lax.rsqrt(jnp.mean(values * values, axis=-1, keepdims=True) + epsilon)
    normed = (values * norm_scale * gain_row).astype(jnp.bfloat16)
    preact = jnp.dot(normed, masked, preferred_element_type=jnp.float32)
    normal_cdf = 0.5 * (1.0 + lax.erf(preact * half_root))
    outputs = (values + preact * normal_cdf).astype(jnp.bfloat16)
    return (normed, preact, outputs)


def section_backward(inputs, preact, upstream, masked, gain_row):
    values = inputs.astype(jnp.float32)
    norm_scale = lax.rsqrt(jnp.mean(values * values, axis=-1, keepdims=True) + epsilon)
    normal_cdf = 0.5 * (1.0 + lax.erf(preact * half_root))
    normal_pdf = jnp.exp(-0.5 * preact * preact) * density_scale
    upstream_f = upstream.astype(jnp.float32)
    grad_pre = (upstream_f * (normal_cdf + preact * normal_pdf)).astype(jnp.bfloat16)
    grad_normed = lax.dot_general(
        grad_pre, masked, (((1,), (1,)), ((), ())), preferred_element_type=jnp.float32
    )
    scaled_grad = grad_normed * gain_row
    grad_input = norm_scale * scaled_grad - values * norm_scale**3 * jnp.mean(
        scaled_grad * values, axis=-1, keepdims=True
    )
    return (grad_pre, (upstream_f + grad_input).astype(jnp.bfloat16))


def write_slot(buffer, new_value, slot_index, is_live):
    old_value = lax.dynamic_index_in_dim(buffer, slot_index, 0, keepdims=False)
    chosen = jnp.where(is_live, new_value, old_value)
    return lax.dynamic_update_index_in_dim(buffer, chosen, slot_index, 0)


def body(activations, cotangent, weight, norm_gain, pair_mask, earlier_mask):
    section_count = lax.axis_size("section")
    replica_count = lax.axis_size("dp")
    section_index = lax.axis_index("section")
    replica_index = lax.axis_index("dp")
    micro_count, row_count, model_width = activations.shape
    shard_rows = weight.shape[1]
    groups = shard_rows // 4
    own_weight = weight[0]
    gain_row = norm_gain[0]
    own_pairs = lax.dynamic_slice_in_dim(pair_mask[0], replica_index * groups, groups, 0)
    own_kept = kept_positions(own_pairs)
    earlier_kept = kept_positions(earlier_mask[0])
    flip_local = jnp.sum(own_kept != earlier_kept).reshape(1)
    flip_sum = of_everyone(flip_local, "dp")
    masked_shard = jnp.where(own_kept, own_weight, jnp.zeros_like(own_weight))
    masked = lax.all_gather(masked_shard, "dp", axis=0, tiled=True)
    tick_count = micro_count + section_count - 1
    act_zeros = jnp.zeros((micro_count, row_count, model_width), jnp.bfloat16)
    stored = (act_zeros,)

    def forward_tick(tick_index, state_tuple):
        received, buffers = state_tuple
        micro_index = tick_index - section_index
        is_live = (micro_index >= 0) & (micro_index < micro_count)
        slot_index = jnp.clip(micro_index, 0, micro_count - 1)
        fresh_rows = lax.dynamic_index_in_dim(activations, slot_index, 0, keepdims=False)
        current = jnp.where(section_index == 0, fresh_rows, received)
        normed, preact, outputs = section_forward(current, masked, gain_row)
        results = (current, normed, preact)
        buffers = tuple(
            (
                write_slot(buffer, update, slot_index, is_live)
                for buffer, update in zip(buffers, results)
            )
        )
        received = shifted(outputs, "section", 1)
        return (received, buffers)

    start_rows = jnp.zeros((row_count, model_width), jnp.bfloat16)
    received, stored = lax.fori_loop(0, tick_count, forward_tick, (start_rows, stored))

    def backward_tick(tick_index, state_tuple):
        received, grad_buffer, normed_buffer = state_tuple
        micro_index = tick_index - (section_count - 1 - section_index)
        is_live = (micro_index >= 0) & (micro_index < micro_count)
        slot_index = jnp.clip(micro_index, 0, micro_count - 1)
        fresh_rows = lax.dynamic_index_in_dim(cotangent, slot_index, 0, keepdims=False)
        upstream = jnp.where(section_index == section_count - 1, fresh_rows, received)
        inputs = lax.dynamic_index_in_dim(stored[0], slot_index, 0, keepdims=False)
        normed, preact, unused = section_forward(inputs, masked, gain_row)
        normed_buffer = write_slot(normed_buffer, normed, slot_index, is_live)
        grad_pre, grad_input = section_backward(inputs, preact, upstream, masked, gain_row)
        grad_buffer = write_slot(grad_buffer, grad_pre, slot_index, is_live)
        received = shifted(grad_input, "section", -1)
        return (received, grad_buffer, normed_buffer)

    received, grad_buffer, normed_buffer = lax.fori_loop(
        0, tick_count, backward_tick, (start_rows, act_zeros, act_zeros)
    )
    flat_normed = normed_buffer.reshape(micro_count * row_count, model_width)
    flat_grad = grad_buffer.reshape(micro_count * row_count, model_width)
    summed = lax.psum_scatter(
        lax.dot_general(
            flat_normed, flat_grad, (((0,), (0,)), ((), ())), preferred_element_type=jnp.float32
        ).astype(jnp.bfloat16),
        "dp",
        scatter_dimension=0,
        tiled=True,
    ).astype(jnp.float32)
    token_total = micro_count * row_count * replica_count
    dense_part = summed / math.sqrt(token_total)
    decay_part = jnp.where(own_kept, 0.0, own_weight.astype(jnp.float32))
    gradient = dense_part + decay_rate * decay_part
    return (gradient[None], flip_sum)


def solution(mesh):
    placed = (
        P(None, "dp", None),
        P(None, "dp", None),
        P("section", "dp", None),
        P("section", None),
        P("section", None, None),
        P("section", "dp", None),
    )
    return jax.shard_map(
        body,
        mesh=mesh,
        in_specs=placed,
        out_specs=(P("section", "dp", None), P("section")),
        check_vma=False,
    )
```

profile of v0, /device:TPU:1, one launch (start us, length us, event | category | flops | bytes accessed | tf_op | source)
XLA Modules:
  0.0 606.8 jit_solution(1059412193560578192)
XLA Ops:
  12.0 62.1 %all-gather.2.cloned.1.call-done = bf16[2048,2048]{1,0:T(8,128)(2,1)} async-done(((bf16[64,2048]{1,0:T(8,128)(2,1)}), bf16[2048,2048]{1,0:T(8,128)(2,1)}) %all-gather.2.cloned.1.call-update) | async-done | bytes 8388624 | tf_op jit(solution)/shard_map/all_gather | solution.py:98
  74.2 160.0 %while.35 = (s32[]{:T(128)}, bf16[64,2048]{1,0:T(8,128)(2,1)S(1)}, bf16[4,64,2048]{2,1,0:T(8,128)(2,1)S(1)}, pred[]{:T(512)}, s32[]{:T(128)}, /*index=5*/bf16[4,...) while((s32[]{:T(128)}, bf16[64,2048]{1,0:T(8,128)(2,1)S(1)}, ...), condition=%wide.region_2.3_spmd, body=%wide.region_0.0_spmd.sunk | while | flops 538968128 | bytes 12068064 | solution.py:122
  75.5 5.1 fusion.69
  83.8 5.4 collective-permute-done
  105.4 5.1 fusion.69
  119.6 5.1 fusion.69
  151.9 5.3 collective-permute-start
  161.7 5.1 fusion.69
  166.8 5.3 collective-permute-start
  191.4 5.1 fusion.69
  206.1 5.1 fusion.69
  235.5 233.0 %while.36 = (s32[]{:T(128)}, bf16[64,2048]{1,0:T(8,128)(2,1)S(1)}, bf16[4,64,2048]{2,1,0:T(8,128)(2,1)S(1)}, bf16[4,64,2048]{2,1,0:T(8,128)(2,1)}, pred[]{:T(512...) while((s32[]{:T(128)}, bf16[64,2048]{1,0:T(8,128)(2,1)S(1)}, ...), condition=%wide.region_6.7_spmd, body=%wide.region_3.6_spmd.sunk | while | flops 1080033536 | bytes 24441880 | solution.py:139
  235.8 5.2 bitcast_dynamic-update-slice_fusion.5
  241.0 6.2 %fusion.73 = (f32[64]{0:T(128)S(1)}, f32[64,2048]{1,0:T(8,128)S(1)}) fusion(bf16[4,64,2048]{2,1,0:T(8,128)(2,1)S(1)} %get-tuple-element.633, s32[]{:T(128)S(6)} %min.21, f32[2048]{0:T(1024)S(1)} %bitcast.96, bf16[2048,2048]{1,0:T(8,128)(2,1)} %get-tuple-element.635, bf16[64,2048]{1,0:T(8,128)(2,1)S(1)} %get-tuple-element.556, ...), kind=kOutput, calls=%fused_computation.32.clone.1 | convolution fusion | flops 538836928 | bytes 9969924 | tf_op jit(solution)/shard_map/while/body/eval_jaxpr/dot_general | solution.py:66
  250.5 5.6 collective-permute-done.1
  256.4 5.2 bitcast_dynamic-update-slice_fusion.5
  261.6 6.2 %fusion.73 = (f32[64]{0:T(128)S(1)}, f32[64,2048]{1,0:T(8,128)S(1)}) fusion(bf16[4,64,2048]{2,1,0:T(8,128)(2,1)S(1)} %get-tuple-element.633, s32[]{:T(128)S(6)} %min.21, f32[2048]{0:T(1024)S(1)} %bitcast.96, bf16[2048,2048]{1,0:T(8,128)(2,1)} %get-tuple-element.635, bf16[64,2048]{1,0:T(8,128)(2,1)S(1)} %get-tuple-element.556, ...), kind=kOutput, calls=%fused_computation.32.clone.1 | convolution fusion | flops 538836928 | bytes 9969924 | tf_op jit(solution)/shard_map/while/body/eval_jaxpr/dot_general | solution.py:66
  271.1 5.6 collective-permute-done.1
  277.0 5.2 bitcast_dynamic-update-slice_fusion.5
  282.2 6.2 %fusion.73 = (f32[64]{0:T(128)S(1)}, f32[64,2048]{1,0:T(8,128)S(1)}) fusion(bf16[4,64,2048]{2,1,0:T(8,128)(2,1)S(1)} %get-tuple-element.633, s32[]{:T(128)S(6)} %min.21, f32[2048]{0:T(1024)S(1)} %bitcast.96, bf16[2048,2048]{1,0:T(8,128)(2,1)} %get-tuple-element.635, bf16[64,2048]{1,0:T(8,128)(2,1)S(1)} %get-tuple-element.556, ...), kind=kOutput, calls=%fused_computation.32.clone.1 | convolution fusion | flops 538836928 | bytes 9969924 | tf_op jit(solution)/shard_map/while/body/eval_jaxpr/dot_general | solution.py:66
  291.8 5.6 collective-permute-done.1
  297.6 5.2 bitcast_dynamic-update-slice_fusion.5
  302.8 6.2 %fusion.73 = (f32[64]{0:T(128)S(1)}, f32[64,2048]{1,0:T(8,128)S(1)}) fusion(bf16[4,64,2048]{2,1,0:T(8,128)(2,1)S(1)} %get-tuple-element.633, s32[]{:T(128)S(6)} %min.21, f32[2048]{0:T(1024)S(1)} %bitcast.96, bf16[2048,2048]{1,0:T(8,128)(2,1)} %get-tuple-element.635, bf16[64,2048]{1,0:T(8,128)(2,1)S(1)} %get-tuple-element.556, ...), kind=kOutput, calls=%fused_computation.32.clone.1 | convolution fusion | flops 538836928 | bytes 9969924 | tf_op jit(solution)/shard_map/while/body/eval_jaxpr/dot_general | solution.py:66
  312.4 5.6 collective-permute-done.1
  318.2 5.2 bitcast_dynamic-update-slice_fusion.5
  323.5 6.2 %fusion.73 = (f32[64]{0:T(128)S(1)}, f32[64,2048]{1,0:T(8,128)S(1)}) fusion(bf16[4,64,2048]{2,1,0:T(8,128)(2,1)S(1)} %get-tuple-element.633, s32[]{:T(128)S(6)} %min.21, f32[2048]{0:T(1024)S(1)} %bitcast.96, bf16[2048,2048]{1,0:T(8,128)(2,1)} %get-tuple-element.635, bf16[64,2048]{1,0:T(8,128)(2,1)S(1)} %get-tuple-element.556, ...), kind=kOutput, calls=%fused_computation.32.clone.1 | convolution fusion | flops 538836928 | bytes 9969924 | tf_op jit(solution)/shard_map/while/body/eval_jaxpr/dot_general | solution.py:66
  333.0 5.2 collective-permute-done.1
  338.4 5.2 bitcast_dynamic-update-slice_fusion.5
  343.6 6.2 %fusion.73 = (f32[64]{0:T(128)S(1)}, f32[64,2048]{1,0:T(8,128)S(1)}) fusion(bf16[4,64,2048]{2,1,0:T(8,128)(2,1)S(1)} %get-tuple-element.633, s32[]{:T(128)S(6)} %min.21, f32[2048]{0:T(1024)S(1)} %bitcast.96, bf16[2048,2048]{1,0:T(8,128)(2,1)} %get-tuple-element.635, bf16[64,2048]{1,0:T(8,128)(2,1)S(1)} %get-tuple-element.556, ...), kind=kOutput, calls=%fused_computation.32.clone.1 | convolution fusion | flops 538836928 | bytes 9969924 | tf_op jit(solution)/shard_map/while/body/eval_jaxpr/dot_general | solution.py:66
  353.2 5.2 collective-permute-done.1
  358.6 5.2 bitcast_dynamic-update-slice_fusion.5
  363.8 6.2 %fusion.73 = (f32[64]{0:T(128)S(1)}, f32[64,2048]{1,0:T(8,128)S(1)}) fusion(bf16[4,64,2048]{2,1,0:T(8,128)(2,1)S(1)} %get-tuple-element.633, s32[]{:T(128)S(6)} %min.21, f32[2048]{0:T(1024)S(1)} %bitcast.96, bf16[2048,2048]{1,0:T(8,128)(2,1)} %get-tuple-element.635, bf16[64,2048]{1,0:T(8,128)(2,1)S(1)} %get-tuple-element.556, ...), kind=kOutput, calls=%fused_computation.32.clone.1 | convolution fusion | flops 538836928 | bytes 9969924 | tf_op jit(solution)/shard_map/while/body/eval_jaxpr/dot_general | solution.py:66
  373.3 5.2 collective-permute-done.1
  378.7 5.2 bitcast_dynamic-update-slice_fusion.5
  384.0 6.2 %fusion.73 = (f32[64]{0:T(128)S(1)}, f32[64,2048]{1,0:T(8,128)S(1)}) fusion(bf16[4,64,2048]{2,1,0:T(8,128)(2,1)S(1)} %get-tuple-element.633, s32[]{:T(128)S(6)} %min.21, f32[2048]{0:T(1024)S(1)} %bitcast.96, bf16[2048,2048]{1,0:T(8,128)(2,1)} %get-tuple-element.635, bf16[64,2048]{1,0:T(8,128)(2,1)S(1)} %get-tuple-element.556, ...), kind=kOutput, calls=%fused_computation.32.clone.1 | convolution fusion | flops 538836928 | bytes 9969924 | tf_op jit(solution)/shard_map/while/body/eval_jaxpr/dot_general | solution.py:66
  393.5 6.1 collective-permute-done.1
  399.8 5.2 bitcast_dynamic-update-slice_fusion.5
  405.0 6.2 %fusion.73 = (f32[64]{0:T(128)S(1)}, f32[64,2048]{1,0:T(8,128)S(1)}) fusion(bf16[4,64,2048]{2,1,0:T(8,128)(2,1)S(1)} %get-tuple-element.633, s32[]{:T(128)S(6)} %min.21, f32[2048]{0:T(1024)S(1)} %bitcast.96, bf16[2048,2048]{1,0:T(8,128)(2,1)} %get-tuple-element.635, bf16[64,2048]{1,0:T(8,128)(2,1)S(1)} %get-tuple-element.556, ...), kind=kOutput, calls=%fused_computation.32.clone.1 | convolution fusion | flops 538836928 | bytes 9969924 | tf_op jit(solution)/shard_map/while/body/eval_jaxpr/dot_general | solution.py:66
  414.5 7.8 %collective-permute-done.1 = bf16[64,2048]{1,0:T(8,128)(2,1)S(1)} collective-permute-done((bf16[64,2048]{1,0:T(8,128)(2,1)S(1)}, bf16[64,2048]{1,0:T(8,128)(2,1)S(1)}, u32[]{:S(2)}, u32[]{:S(2)}) %collective-permute-start.1) | collective-permute-done | bytes 262176 | tf_op jit(solution)/shard_map/while/body/eval_jaxpr/ppermute | solution.py:28
  422.5 5.2 bitcast_dynamic-update-slice_fusion.5
  427.7 6.2 %fusion.73 = (f32[64]{0:T(128)S(1)}, f32[64,2048]{1,0:T(8,128)S(1)}) fusion(bf16[4,64,2048]{2,1,0:T(8,128)(2,1)S(1)} %get-tuple-element.633, s32[]{:T(128)S(6)} %min.21, f32[2048]{0:T(1024)S(1)} %bitcast.96, bf16[2048,2048]{1,0:T(8,128)(2,1)} %get-tuple-element.635, bf16[64,2048]{1,0:T(8,128)(2,1)S(1)} %get-tuple-element.556, ...), kind=kOutput, calls=%fused_computation.32.clone.1 | convolution fusion | flops 538836928 | bytes 9969924 | tf_op jit(solution)/shard_map/while/body/eval_jaxpr/dot_general | solution.py:66
  437.3 8.8 %collective-permute-done.1 = bf16[64,2048]{1,0:T(8,128)(2,1)S(1)} collective-permute-done((bf16[64,2048]{1,0:T(8,128)(2,1)S(1)}, bf16[64,2048]{1,0:T(8,128)(2,1)S(1)}, u32[]{:S(2)}, u32[]{:S(2)}) %collective-permute-start.1) | collective-permute-done | bytes 262176 | tf_op jit(solution)/shard_map/while/body/eval_jaxpr/ppermute | solution.py:28
  446.2 5.2 bitcast_dynamic-update-slice_fusion.5
  451.5 6.2 %fusion.73 = (f32[64]{0:T(128)S(1)}, f32[64,2048]{1,0:T(8,128)S(1)}) fusion(bf16[4,64,2048]{2,1,0:T(8,128)(2,1)S(1)} %get-tuple-element.633, s32[]{:T(128)S(6)} %min.21, f32[2048]{0:T(1024)S(1)} %bitcast.96, bf16[2048,2048]{1,0:T(8,128)(2,1)} %get-tuple-element.635, bf16[64,2048]{1,0:T(8,128)(2,1)S(1)} %get-tuple-element.556, ...), kind=kOutput, calls=%fused_computation.32.clone.1 | convolution fusion | flops 538836928 | bytes 9969924 | tf_op jit(solution)/shard_map/while/body/eval_jaxpr/dot_general | solution.py:66
  461.0 7.5 %collective-permute-done.1 = bf16[64,2048]{1,0:T(8,128)(2,1)S(1)} collective-permute-done((bf16[64,2048]{1,0:T(8,128)(2,1)S(1)}, bf16[64,2048]{1,0:T(8,128)(2,1)S(1)}, u32[]{:S(2)}, u32[]{:S(2)}) %collective-permute-start.1) | collective-permute-done | bytes 262176 | tf_op jit(solution)/shard_map/while/body/eval_jaxpr/ppermute | solution.py:28
  468.5 6.8 %bitcast_convert_fusion = bf16[2048,2048]{1,0:T(8,128)(2,1)} fusion(bf16[4,64,2048]{2,1,0:T(8,128)(2,1)} %get-tuple-element.378, bf16[4,64,2048]{2,1,0:T(8,128)(2,1)S(1)} %get-tuple-element.379), kind=kOutput, calls=%fused_computation.63 | convolution fusion | flops 2151677952 | bytes 10485760 | tf_op jit(solution)/shard_map/dot_general | solution.py:145
  477.0 35.0 %all_to_all.6 = s32[32,1,1]{2,1,0:T(1,128)S(1)} all-to-all(s32[32,1,1]{2,1,0:T(1,128)S(1)} %broadcast_in_dim.94), channel_id=1, replica_groups=mesh['dp'=32,'section'=8] {'dp'}, dimensions={0} | all-to-all | bytes 256 | tf_op jit(solution)/shard_map/all_to_all | solution.py:18
  512.7 85.4 %reduce-scatter.2.cloned.1.call-done = bf16[64,2048]{1,0:T(8,128)(2,1)} async-done(((bf16[2048,2048]{1,0:T(8,128)(2,1)}), bf16[64,2048]{1,0:T(8,128)(2,1)}) %reduce-scatter.2.cloned.1.call-update) | async-done | bytes 262160 | tf_op jit(solution)/shard_map/reduce_scatter | solution.py:144
  (191 shorter events, 162.4 us)
Async XLA Ops:
  7.2 66.9 %all-gather.2.cloned.1.call-start = ((), (), s32[]{:S(2)}) async-start(), calls=%async_computation.2 | async-start | bytes 8650752 | tf_op jit(solution)/shard_map/all_gather | solution.py:98
  11.9 586.2 %reduce-scatter.2.cloned.1.call-start = ((), (), s32[]{:S(2)}) async-start(), calls=%async_computation.3 | async-start | bytes 8650752 | tf_op jit(solution)/shard_map/reduce_scatter | solution.py:144
  80.6 8.6 %collective-permute-start = (bf16[64,2048]{1,0:T(8,128)(2,1)S(1)}, bf16[64,2048]{1,0:T(8,128)(2,1)S(1)}, u32[]{:S(2)}, u32[]{:S(2)}) collective-permute-start(bf16[64,2048]{1,0:T(8,128)(2,1)S(1)} %fusion.69), channel_id=1, source_target_pairs={{0,1},{1,2},{2,3},{3,4},{4,5},{5,6},{6,7},{8,9},{9,10},{10,11},{11... | collective-permute-start | bytes 786440 | tf_op jit(solution)/shard_map/while/body/eval_jaxpr/ppermute | solution.py:28
  95.5 8.6 %collective-permute-start = (bf16[64,2048]{1,0:T(8,128)(2,1)S(1)}, bf16[64,2048]{1,0:T(8,128)(2,1)S(1)}, u32[]{:S(2)}, u32[]{:S(2)}) collective-permute-start(bf16[64,2048]{1,0:T(8,128)(2,1)S(1)} %fusion.69), channel_id=1, source_target_pairs={{0,1},{1,2},{2,3},{3,4},{4,5},{5,6},{6,7},{8,9},{9,10},{10,11},{11... | collective-permute-start | bytes 786440 | tf_op jit(solution)/shard_map/while/body/eval_jaxpr/ppermute | solution.py:28
  110.5 7.8 %collective-permute-start = (bf16[64,2048]{1,0:T(8,128)(2,1)S(1)}, bf16[64,2048]{1,0:T(8,128)(2,1)S(1)}, u32[]{:S(2)}, u32[]{:S(2)}) collective-permute-start(bf16[64,2048]{1,0:T(8,128)(2,1)S(1)} %fusion.69), channel_id=1, source_target_pairs={{0,1},{1,2},{2,3},{3,4},{4,5},{5,6},{6,7},{8,9},{9,10},{10,11},{11... | collective-permute-start | bytes 786440 | tf_op jit(solution)/shard_map/while/body/eval_jaxpr/ppermute | solution.py:28
  124.7 7.4 %collective-permute-start = (bf16[64,2048]{1,0:T(8,128)(2,1)S(1)}, bf16[64,2048]{1,0:T(8,128)(2,1)S(1)}, u32[]{:S(2)}, u32[]{:S(2)}) collective-permute-start(bf16[64,2048]{1,0:T(8,128)(2,1)S(1)} %fusion.69), channel_id=1, source_target_pairs={{0,1},{1,2},{2,3},{3,4},{4,5},{5,6},{6,7},{8,9},{9,10},{10,11},{11... | collective-permute-start | bytes 786440 | tf_op jit(solution)/shard_map/while/body/eval_jaxpr/ppermute | solution.py:28
  138.4 7.1 %collective-permute-start = (bf16[64,2048]{1,0:T(8,128)(2,1)S(1)}, bf16[64,2048]{1,0:T(8,128)(2,1)S(1)}, u32[]{:S(2)}, u32[]{:S(2)}) collective-permute-start(bf16[64,2048]{1,0:T(8,128)(2,1)S(1)} %fusion.69), channel_id=1, source_target_pairs={{0,1},{1,2},{2,3},{3,4},{4,5},{5,6},{6,7},{8,9},{9,10},{10,11},{11... | collective-permute-start | bytes 786440 | tf_op jit(solution)/shard_map/while/body/eval_jaxpr/ppermute | solution.py:28
  151.9 8.5 %collective-permute-start = (bf16[64,2048]{1,0:T(8,128)(2,1)S(1)}, bf16[64,2048]{1,0:T(8,128)(2,1)S(1)}, u32[]{:S(2)}, u32[]{:S(2)}) collective-permute-start(bf16[64,2048]{1,0:T(8,128)(2,1)S(1)} %fusion.69), channel_id=1, source_target_pairs={{0,1},{1,2},{2,3},{3,4},{4,5},{5,6},{6,7},{8,9},{9,10},{10,11},{11... | collective-permute-start | bytes 786440 | tf_op jit(solution)/shard_map/while/body/eval_jaxpr/ppermute | solution.py:28
  166.8 8.6 %collective-permute-start = (bf16[64,2048]{1,0:T(8,128)(2,1)S(1)}, bf16[64,2048]{1,0:T(8,128)(2,1)S(1)}, u32[]{:S(2)}, u32[]{:S(2)}) collective-permute-start(bf16[64,2048]{1,0:T(8,128)(2,1)S(1)} %fusion.69), channel_id=1, source_target_pairs={{0,1},{1,2},{2,3},{3,4},{4,5},{5,6},{6,7},{8,9},{9,10},{10,11},{11... | collective-permute-start | bytes 786440 | tf_op jit(solution)/shard_map/while/body/eval_jaxpr/ppermute | solution.py:28
  181.8 8.3 %collective-permute-start = (bf16[64,2048]{1,0:T(8,128)(2,1)S(1)}, bf16[64,2048]{1,0:T(8,128)(2,1)S(1)}, u32[]{:S(2)}, u32[]{:S(2)}) collective-permute-start(bf16[64,2048]{1,0:T(8,128)(2,1)S(1)} %fusion.69), channel_id=1, source_target_pairs={{0,1},{1,2},{2,3},{3,4},{4,5},{5,6},{6,7},{8,9},{9,10},{10,11},{11... | collective-permute-start | bytes 786440 | tf_op jit(solution)/shard_map/while/body/eval_jaxpr/ppermute | solution.py:28
  196.5 8.3 %collective-permute-start = (bf16[64,2048]{1,0:T(8,128)(2,1)S(1)}, bf16[64,2048]{1,0:T(8,128)(2,1)S(1)}, u32[]{:S(2)}, u32[]{:S(2)}) collective-permute-start(bf16[64,2048]{1,0:T(8,128)(2,1)S(1)} %fusion.69), channel_id=1, source_target_pairs={{0,1},{1,2},{2,3},{3,4},{4,5},{5,6},{6,7},{8,9},{9,10},{10,11},{11... | collective-permute-start | bytes 786440 | tf_op jit(solution)/shard_map/while/body/eval_jaxpr/ppermute | solution.py:28
  211.2 8.3 %collective-permute-start = (bf16[64,2048]{1,0:T(8,128)(2,1)S(1)}, bf16[64,2048]{1,0:T(8,128)(2,1)S(1)}, u32[]{:S(2)}, u32[]{:S(2)}) collective-permute-start(bf16[64,2048]{1,0:T(8,128)(2,1)S(1)} %fusion.69), channel_id=1, source_target_pairs={{0,1},{1,2},{2,3},{3,4},{4,5},{5,6},{6,7},{8,9},{9,10},{10,11},{11... | collective-permute-start | bytes 786440 | tf_op jit(solution)/shard_map/while/body/eval_jaxpr/ppermute | solution.py:28
  225.9 8.3 %collective-permute-start = (bf16[64,2048]{1,0:T(8,128)(2,1)S(1)}, bf16[64,2048]{1,0:T(8,128)(2,1)S(1)}, u32[]{:S(2)}, u32[]{:S(2)}) collective-permute-start(bf16[64,2048]{1,0:T(8,128)(2,1)S(1)} %fusion.69), channel_id=1, source_target_pairs={{0,1},{1,2},{2,3},{3,4},{4,5},{5,6},{6,7},{8,9},{9,10},{10,11},{11... | collective-permute-start | bytes 786440 | tf_op jit(solution)/shard_map/while/body/eval_jaxpr/ppermute | solution.py:28
  235.7 5.2 copy-start
  247.4 8.8 %collective-permute-start.1 = (bf16[64,2048]{1,0:T(8,128)(2,1)S(1)}, bf16[64,2048]{1,0:T(8,128)(2,1)S(1)}, u32[]{:S(2)}, u32[]{:S(2)}) collective-permute-start(bf16[64,2048]{1,0:T(8,128)(2,1)S(1)} %fusion.74), channel_id=1, source_target_pairs={{1,0},{2,1},{3,2},{4,3},{5,4},{6,5},{7,6},{9,8},{10,9},{11,10},{12... | collective-permute-start | bytes 786440 | tf_op jit(solution)/shard_map/while/body/eval_jaxpr/ppermute | solution.py:28
  256.4 5.2 copy-start
  268.0 8.8 %collective-permute-start.1 = (bf16[64,2048]{1,0:T(8,128)(2,1)S(1)}, bf16[64,2048]{1,0:T(8,128)(2,1)S(1)}, u32[]{:S(2)}, u32[]{:S(2)}) collective-permute-start(bf16[64,2048]{1,0:T(8,128)(2,1)S(1)} %fusion.74), channel_id=1, source_target_pairs={{1,0},{2,1},{3,2},{4,3},{5,4},{6,5},{7,6},{9,8},{10,9},{11,10},{12... | collective-permute-start | bytes 786440 | tf_op jit(solution)/shard_map/while/body/eval_jaxpr/ppermute | solution.py:28
  277.0 5.2 copy-start
  288.6 8.8 %collective-permute-start.1 = (bf16[64,2048]{1,0:T(8,128)(2,1)S(1)}, bf16[64,2048]{1,0:T(8,128)(2,1)S(1)}, u32[]{:S(2)}, u32[]{:S(2)}) collective-permute-start(bf16[64,2048]{1,0:T(8,128)(2,1)S(1)} %fusion.74), channel_id=1, source_target_pairs={{1,0},{2,1},{3,2},{4,3},{5,4},{6,5},{7,6},{9,8},{10,9},{11,10},{12... | collective-permute-start | bytes 786440 | tf_op jit(solution)/shard_map/while/body/eval_jaxpr/ppermute | solution.py:28
  297.6 5.2 copy-start
  309.2 8.8 %collective-permute-start.1 = (bf16[64,2048]{1,0:T(8,128)(2,1)S(1)}, bf16[64,2048]{1,0:T(8,128)(2,1)S(1)}, u32[]{:S(2)}, u32[]{:S(2)}) collective-permute-start(bf16[64,2048]{1,0:T(8,128)(2,1)S(1)} %fusion.74), channel_id=1, source_target_pairs={{1,0},{2,1},{3,2},{4,3},{5,4},{6,5},{7,6},{9,8},{10,9},{11,10},{12... | collective-permute-start | bytes 786440 | tf_op jit(solution)/shard_map/while/body/eval_jaxpr/ppermute | solution.py:28
  318.2 5.2 copy-start
  329.9 8.3 %collective-permute-start.1 = (bf16[64,2048]{1,0:T(8,128)(2,1)S(1)}, bf16[64,2048]{1,0:T(8,128)(2,1)S(1)}, u32[]{:S(2)}, u32[]{:S(2)}) collective-permute-start(bf16[64,2048]{1,0:T(8,128)(2,1)S(1)} %fusion.74), channel_id=1, source_target_pairs={{1,0},{2,1},{3,2},{4,3},{5,4},{6,5},{7,6},{9,8},{10,9},{11,10},{12... | collective-permute-start | bytes 786440 | tf_op jit(solution)/shard_map/while/body/eval_jaxpr/ppermute | solution.py:28
  338.4 5.2 copy-start
  350.0 8.3 %collective-permute-start.1 = (bf16[64,2048]{1,0:T(8,128)(2,1)S(1)}, bf16[64,2048]{1,0:T(8,128)(2,1)S(1)}, u32[]{:S(2)}, u32[]{:S(2)}) collective-permute-start(bf16[64,2048]{1,0:T(8,128)(2,1)S(1)} %fusion.74), channel_id=1, source_target_pairs={{1,0},{2,1},{3,2},{4,3},{5,4},{6,5},{7,6},{9,8},{10,9},{11,10},{12... | collective-permute-start | bytes 786440 | tf_op jit(solution)/shard_map/while/body/eval_jaxpr/ppermute | solution.py:28
  358.5 5.2 copy-start
  370.2 8.3 %collective-permute-start.1 = (bf16[64,2048]{1,0:T(8,128)(2,1)S(1)}, bf16[64,2048]{1,0:T(8,128)(2,1)S(1)}, u32[]{:S(2)}, u32[]{:S(2)}) collective-permute-start(bf16[64,2048]{1,0:T(8,128)(2,1)S(1)} %fusion.74), channel_id=1, source_target_pairs={{1,0},{2,1},{3,2},{4,3},{5,4},{6,5},{7,6},{9,8},{10,9},{11,10},{12... | collective-permute-start | bytes 786440 | tf_op jit(solution)/shard_map/while/body/eval_jaxpr/ppermute | solution.py:28
  378.7 5.2 copy-start
  390.4 9.2 %collective-permute-start.1 = (bf16[64,2048]{1,0:T(8,128)(2,1)S(1)}, bf16[64,2048]{1,0:T(8,128)(2,1)S(1)}, u32[]{:S(2)}, u32[]{:S(2)}) collective-permute-start(bf16[64,2048]{1,0:T(8,128)(2,1)S(1)} %fusion.74), channel_id=1, source_target_pairs={{1,0},{2,1},{3,2},{4,3},{5,4},{6,5},{7,6},{9,8},{10,9},{11,10},{12... | collective-permute-start | bytes 786440 | tf_op jit(solution)/shard_map/while/body/eval_jaxpr/ppermute | solution.py:28
  399.8 5.2 copy-start
  411.4 10.9 %collective-permute-start.1 = (bf16[64,2048]{1,0:T(8,128)(2,1)S(1)}, bf16[64,2048]{1,0:T(8,128)(2,1)S(1)}, u32[]{:S(2)}, u32[]{:S(2)}) collective-permute-start(bf16[64,2048]{1,0:T(8,128)(2,1)S(1)} %fusion.74), channel_id=1, source_target_pairs={{1,0},{2,1},{3,2},{4,3},{5,4},{6,5},{7,6},{9,8},{10,9},{11,10},{12... | collective-permute-start | bytes 786440 | tf_op jit(solution)/shard_map/while/body/eval_jaxpr/ppermute | solution.py:28
  422.5 5.2 copy-start
  434.1 11.9 %collective-permute-start.1 = (bf16[64,2048]{1,0:T(8,128)(2,1)S(1)}, bf16[64,2048]{1,0:T(8,128)(2,1)S(1)}, u32[]{:S(2)}, u32[]{:S(2)}) collective-permute-start(bf16[64,2048]{1,0:T(8,128)(2,1)S(1)} %fusion.74), channel_id=1, source_target_pairs={{1,0},{2,1},{3,2},{4,3},{5,4},{6,5},{7,6},{9,8},{10,9},{11,10},{12... | collective-permute-start | bytes 786440 | tf_op jit(solution)/shard_map/while/body/eval_jaxpr/ppermute | solution.py:28
  446.2 5.2 copy-start
  457.9 10.6 %collective-permute-start.1 = (bf16[64,2048]{1,0:T(8,128)(2,1)S(1)}, bf16[64,2048]{1,0:T(8,128)(2,1)S(1)}, u32[]{:S(2)}, u32[]{:S(2)}) collective-permute-start(bf16[64,2048]{1,0:T(8,128)(2,1)S(1)} %fusion.74), channel_id=1, source_target_pairs={{1,0},{2,1},{3,2},{4,3},{5,4},{6,5},{7,6},{9,8},{10,9},{11,10},{12... | collective-permute-start | bytes 786440 | tf_op jit(solution)/shard_map/while/body/eval_jaxpr/ppermute | solution.py:28
  475.3 122.8 %copy-start.1 = (bf16[1,64,2048]{2,1,0:T(8,128)(2,1)S(1)}, bf16[1,64,2048]{2,1,0:T(8,128)(2,1)}, u32[]{:S(2)}) copy-start(bf16[1,64,2048]{2,1,0:T(8,128)(2,1)} %param.12) | copy-start | bytes 786436
Sparse Core Ops, SparseCore 0:
  12.1 61.9 all-gather.1
  475.5 122.5 reduce-scatter.1
where the time goes:
time: 610 us; the launch traced here: 607 us
  waiting for transfers between devices  255 us (42%)
  matrix products  188 us (31%)
  starting transfers between devices  64.4 us (11%)
  other arithmetic  45.4 us (7%)
  blocking collectives  35 us (6%)
  between operations  14.1 us (2%)
    dot_general x22, matrix products, section_forward(): preact = jnp.dot(normed, masked, preferred_element_type=jnp.float32)  113 us
    ppermute x22, waiting for transfers between devices, shifted(): return lax.ppermute(block, axis, route)  108 us
    reduce_scatter x1, waiting for transfers between devices, body(): lax.psum_scatter(lax.dot_general(flat_normed, flat_grad, (((0,), (0,)), (...  85.4 us
    dot_general x11, matrix products, section_backward(): lax.dot_general(grad_pre, masked, (((1,), (1,)), ((), ())), preferred_ele...  67.8 us
    ppermute x22, starting transfers between devices, shifted(): return lax.ppermute(block, axis, route)  64.3 us
    all_gather x1, waiting for transfers between devices, body(): masked = lax.all_gather(masked_shard, 'dp', axis=0, tiled=True)  62.1 us
    all_to_all x1, blocking collectives, copy_for_each(): return lax.all_to_all(copies, axis, split_axis=0, concat_axis=0, tiled=True)  35 us
    dynamic_update_slice x22, other arithmetic, write_slot(): return lax.dynamic_update_index_in_dim(buffer, chosen, slot_index, 0)  32 us
  transfers between devices with their start and end apart: 24, of which 24 were waited for; matrix products, arithmetic and copies ran while one was open for 4% of the time, Pallas kernels for 0%

commit v1 on v0

v1 whole, which is shorter than its diff:
```python
import functools
import math

import jax
import jax.numpy as jnp
from jax import lax
from jax.experimental import pallas as pl
from jax.experimental.pallas import tpu as pltpu
from jax.sharding import PartitionSpec as P

MESH = pl.DeviceIdType.MESH
epsilon = 1e-06
decay_rate = 4.0
half_root = 0.7071067811865476
density_scale = 0.3989422804014327
first_table = (0, 0, 0, 1, 1, 2)
second_table = (1, 2, 3, 2, 3, 3)
BF = jnp.bfloat16
F32 = jnp.float32


def pair_ends(indices):
    leading = jnp.zeros_like(indices)
    trailing = jnp.zeros_like(indices)
    for pair_index in range(6):
        matches = indices == pair_index
        leading = jnp.where(matches, first_table[pair_index], leading)
        trailing = jnp.where(matches, second_table[pair_index], trailing)
    return (leading, trailing)


def kept_positions(indices):
    leading, trailing = pair_ends(indices)
    groups, columns = indices.shape
    positions = lax.broadcasted_iota(jnp.int32, (groups, 4, columns), 1)
    kept_mask = (positions == leading[:, None, :]) | (positions == trailing[:, None, :])
    return kept_mask.reshape(groups * 4, columns)


def pipeline_kernel(micros, sections, x_hbm, ct_hbm, w_hbm, gain_ref, out_ref, w, hin, gin, hout, gout,
                    preact, slope, normed, grad_pre, scale, w_sem, x_sem, f_send, f_recv, b_send, b_recv):
    s = lax.axis_index("section")
    last = sections - 1
    rows_all, width = hin.shape
    rows = rows_all // micros
    chunk = min(512, width)
    chunks = width // chunk

    first_stage, last_stage = s == 0, s == last
    w_copies = [
        pltpu.make_async_copy(w_hbm.at[pl.ds(k * chunk, chunk)], w.at[pl.ds(k * chunk, chunk)], w_sem.at[k])
        for k in range(chunks)
    ]
    for copy in w_copies:
        copy.start()
    x_copy = pltpu.make_async_copy(x_hbm, hin, x_sem.at[0])
    ct_copy = pltpu.make_async_copy(ct_hbm, gin, x_sem.at[1])

    @pl.when(first_stage)
    def _():
        x_copy.start()

    @pl.when(last_stage)
    def _():
        ct_copy.start()

    barrier = pltpu.get_barrier_semaphore()

    @pl.when(s > 0)
    def _():
        pl.semaphore_signal(barrier, inc=1, device_id={"section": s - 1}, device_id_type=MESH)

    @pl.when(s < last)
    def _():
        pl.semaphore_signal(barrier, inc=1, device_id={"section": s + 1}, device_id_type=MESH)

    pl.semaphore_wait(barrier, jnp.where(s > 0, 1, 0) + jnp.where(s < last, 1, 0))

    for copy in w_copies:
        copy.wait()

    @pl.when(first_stage)
    def _():
        x_copy.wait()

    @pl.when(last_stage)
    def _():
        ct_copy.wait()

    def forward_copy(m, where):
        return pltpu.make_async_remote_copy(
            src_ref=hout.at[where], dst_ref=hin.at[where], send_sem=f_send.at[m], recv_sem=f_recv.at[m],
            device_id={"section": jnp.minimum(s + 1, last)}, device_id_type=MESH)

    def backward_copy(m, where):
        return pltpu.make_async_remote_copy(
            src_ref=gout.at[where], dst_ref=gin.at[where], send_sem=b_send.at[m], recv_sem=b_recv.at[m],
            device_id={"section": jnp.maximum(s - 1, 0)}, device_id_type=MESH)

    gain = gain_ref[...]

    def forward(m, carry):
        at = pl.ds(pl.multiple_of(m * rows, rows), rows)

        @pl.when(s > 0)
        def _():
            forward_copy(m, (at,)).wait_recv()

        values = hin[at, :].astype(F32)
        q = lax.rsqrt(jnp.sum(values * values, axis=-1, keepdims=True) * (1.0 / width) + epsilon)
        scale[at, :] = jnp.broadcast_to(q, (rows, 128))
        normal = (values * q * gain).astype(BF)
        normed[at, :] = normal
        for c in range(chunks):
            cols = pl.ds(c * chunk, chunk)
            p = jnp.dot(normal, w[:, cols], preferred_element_type=F32)
            cdf = 0.5 * (1.0 + lax.erf(p * half_root))
            hout[at, cols] = (hin[at, cols].astype(F32) + p * cdf).astype(BF)

            @pl.when(s < last)
            def _():
                forward_copy(m, (at, cols)).start()

            preact[at, cols] = p
            slope[at, cols] = cdf + p * (jnp.exp(-0.5 * p * p) * density_scale)
        return carry

    lax.fori_loop(0, micros, forward, 0)

    def backward(m, carry):
        at = pl.ds(pl.multiple_of(m * rows, rows), rows)

        @pl.when(s < last)
        def _():
            backward_copy(m, (at,)).wait_recv()

        gp = (gin[at, :].astype(F32) * slope[at, :]).astype(BF)
        grad_pre[at, :] = gp
        q = scale[at, 0:1]
        mean = jnp.sum(gp.astype(F32) * preact[at, :], axis=-1, keepdims=True) * (1.0 / width)
        pull = q * q * mean

        @pl.when(s > 0)
        def _():
            for c in range(chunks):
                cols = pl.ds(c * chunk, chunk)
                a = lax.dot_general(gp, w[cols, :], (((1,), (1,)), ((), ())), preferred_element_type=F32)
                a = a * gain_ref[:, cols]
                gout[at, cols] = (gin[at, cols].astype(F32) + q * a - hin[at, cols].astype(F32) * pull).astype(BF)
                backward_copy(m, (at, cols)).start()
        return carry

    lax.fori_loop(0, micros, backward, 0)

    tile = 256 if width % 256 == 0 else 128

    def terms(i, carry):
        cols = pl.ds(pl.multiple_of(i * tile, tile), tile)
        out_ref[cols, :] = lax.dot_general(
            normed[:, cols], grad_pre[...], (((0,), (0,)), ((), ())), preferred_element_type=F32).astype(BF)
        return carry

    lax.fori_loop(0, width // tile, terms, 0)

    def drain(m, carry):
        at = pl.ds(pl.multiple_of(m * rows, rows), rows)

        @pl.when(s < last)
        def _():
            forward_copy(m, (at,)).wait_send()

        @pl.when(s > 0)
        def _():
            backward_copy(m, (at,)).wait_send()

        return carry

    lax.fori_loop(0, micros, drain, 0)


def pipeline(x, ct, masked, gain, sections, micros):
    rows, width = x.shape
    chunks = width // min(512, width)
    vmem = pl.BlockSpec(memory_space=pltpu.VMEM)
    hbm = pl.BlockSpec(memory_space=pl.ANY)
    act = pltpu.VMEM((rows, width), BF)
    wide = pltpu.VMEM((rows, width), F32)
    dma = pltpu.SemaphoreType.DMA
    return pl.pallas_call(
        functools.partial(pipeline_kernel, micros, sections),
        out_shape=jax.ShapeDtypeStruct((width, width), BF),
        in_specs=[hbm, hbm, hbm, vmem],
        out_specs=vmem,
        scratch_shapes=[
            pltpu.VMEM((width, width), BF), act, act, act, act, wide, wide, act, act, pltpu.VMEM((rows, 128), F32),
            dma((chunks,)), dma((2,)), dma((micros,)), dma((micros,)), dma((micros,)), dma((micros,)),
        ],
        compiler_params=pltpu.CompilerParams(
            collective_id=0, has_side_effects=True, vmem_limit_bytes=48 * 1024 * 1024),
        cost_estimate=pl.CostEstimate(
            flops=6 * rows * width * width, bytes_accessed=4 * width * width, transcendentals=0),
    )(x, ct, masked, gain)


def body(activations, cotangent, weight, norm_gain, pair_mask, earlier_mask):
    section_count = lax.axis_size("section")
    replica_count = lax.axis_size("dp")
    replica_index = lax.axis_index("dp")
    micro_count, row_count, model_width = activations.shape
    shard_rows = weight.shape[1]
    groups = shard_rows // 4
    own_weight = weight[0]
    own_pairs = lax.dynamic_slice_in_dim(pair_mask[0], replica_index * groups, groups, 0)
    own_kept = kept_positions(own_pairs)
    earlier_kept = kept_positions(earlier_mask[0])
    flip_local = jnp.sum(own_kept != earlier_kept).reshape(1)
    flip_sum = lax.psum(flip_local, "dp")
    masked_shard = jnp.where(own_kept, own_weight, jnp.zeros_like(own_weight))
    masked = lax.all_gather(masked_shard, "dp", axis=0, tiled=True)
    tokens = micro_count * row_count
    partial = pipeline(
        activations.reshape(tokens, model_width), cotangent.reshape(tokens, model_width), masked, norm_gain,
        section_count, 8)
    summed = lax.psum_scatter(partial, "dp", scatter_dimension=0, tiled=True).astype(jnp.float32)
    dense_part = summed / math.sqrt(tokens * replica_count)
    decay_part = jnp.where(own_kept, 0.0, own_weight.astype(jnp.float32))
    gradient = dense_part + decay_rate * decay_part
    return (gradient[None], flip_sum)


def solution(mesh):
    placed = (
        P(None, "dp", None),
        P(None, "dp", None),
        P("section", "dp", None),
        P("section", None),
        P("section", None, None),
        P("section", "dp", None),
    )
    return jax.shard_map(
        body,
        mesh=mesh,
        in_specs=placed,
        out_specs=(P("section", "dp", None), P("section")),
        check_vma=False,
    )
```

time: 610 us -> 315 us (0.52)
  matrix products: 188 us -> 0 us
  Pallas kernels: 0 us -> 128 us
  waiting for transfers between devices: 255 us -> 141 us
  starting transfers between devices: 64.4 us -> 0.08 us
  other arithmetic: 45.4 us -> 8.5 us
  blocking collectives: 35 us -> 19.4 us
    dot_general x34 -> x0, matrix products: 188 us -> none  [the longest x22 113 us: section_forward(): preact = jnp.dot(normed, masked, preferred_element_type=jnp.float32)]
    pallas_call x0 -> x1, Pallas kernels: none -> 128 us  [pipeline(): pl.pallas_call(functools.partial(pipeline_kernel, micros, sections), out_...]
    ppermute x22 -> x0, waiting for transfers between devices: 108 us -> none  [shifted(): return lax.ppermute(block, axis, route)]
    ppermute x22 -> x0, starting transfers between devices: 64.3 us -> none  [shifted(): return lax.ppermute(block, axis, route)]
    all_to_all x1 -> x0, blocking collectives: 35 us -> none  [copy_for_each(): return lax.all_to_all(copies, axis, split_axis=0, concat_axis=0, tiled=True)]
    dynamic_update_slice x22 -> x0, other arithmetic: 32 us -> none  [write_slot(): return lax.dynamic_update_index_in_dim(buffer, chosen, slot_index, 0)]
    psum x0 -> x1, blocking collectives: none -> 19.4 us  [body(): flip_sum = lax.psum(flip_local, 'dp')]
    reduce_scatter x1, waiting for transfers between devices: 85.4 us -> 79.3 us  [body(): lax.psum_scatter(partial, 'dp', scatter_dimension=0, tiled=True)]
  transfers between devices with their start and end apart: 24 -> 2, of which waited for: 24 -> 2; matrix products, arithmetic and copies ran while one was open for 4% -> 0% of each run, Pallas kernels for 0% -> 0%
where the time goes in v1:
time: 315 us; the launch traced here: 314 us
  waiting for transfers between devices  141 us (45%)
  Pallas kernels  128 us (41%)
  blocking collectives  19.4 us (6%)
  between operations  14.1 us (4%)
  other arithmetic  8.5 us (3%)
    pallas_call x1, Pallas kernels, pipeline(): pl.pallas_call(functools.partial(pipeline_kernel, micros, sections), out_...  128 us
    reduce_scatter x1, waiting for transfers between devices, body(): lax.psum_scatter(partial, 'dp', scatter_dimension=0, tiled=True)  79.3 us
    all_gather x1, waiting for transfers between devices, body(): masked = lax.all_gather(masked_shard, 'dp', axis=0, tiled=True)  62.1 us
    psum x1, blocking collectives, body(): flip_sum = lax.psum(flip_local, 'dp')  19.4 us
  transfers between devices with their start and end apart: 2, of which 2 were waited for; matrix products, arithmetic and copies ran while one was open for 0% of the time, Pallas kernels for 0%

profile of v1, /device:TPU:1, one launch (start us, length us, event | category | flops | bytes accessed | tf_op | source)
XLA Modules:
  0.0 314.0 jit_solution(17143090807922666879)
XLA Ops:
  7.2 0.0 copy-start.2
  7.2 0.0 copy-start.1
  7.2 0.0 copy-start
  7.2 0.0 all-gather.2.cloned.1.call-start
  7.3 0.1 iota.38
  7.3 1.7 select_bitcast_fusion.3
  9.1 0.1 eq.180
  9.2 0.2 eq.181
  9.4 1.8 select_bitcast_fusion.1
  11.2 0.1 eq.186
  11.3 1.0 eq.187
  12.3 2.1 bitcast_select_fusion
  14.4 0.0 all-gather.2.cloned.1.call-update
  14.4 0.0 reduce-scatter.2.cloned.1.call-start
  14.5 62.1 %all-gather.2.cloned.1.call-done.w_hbm = bf16[2048,2048]{1,0:T(8,128)(2,1)} async-done(((bf16[64,2048]{1,0:T(8,128)(2,1)}), bf16[2048,2048]{1,0:T(8,128)(2,1)}) %all-gather.2.cloned.1.call-update) | async-done | bytes 8388624 | tf_op jit(solution)/shard_map/all_gather | solution.py:219
  76.6 0.0 copy-done.2
  76.6 0.0 copy-done.1
  76.6 0.0 copy-done
  76.6 128.1 %shard_map.77 = bf16[2048,2048]{1,0:T(8,128)(2,1)} custom-call(bf16[256,2048]{1,0:T(8,128)(2,1)S(1)} %bitcast.16, bf16[256,2048]{1,0:T(8,128)(2,1)S(1)} %bitcast.17, bf16[2048,2048]{1,0:T(8,128)(2,1)} %all-gather.2.cloned.1.call-done.w_hbm, f32[1,2048]{1,0:T(1,128)S(1)} %copy-done.2), custom_call_target="tpu_custom_call" | custom-call | flops 6442450944 | bytes 16777216 | tf_op jit(solution)/shard_map/pallas_call | solution.py:189
  204.7 0.0 copy-start.4
  204.7 0.0 copy-start.3
  204.7 0.0 reduce-scatter.2.cloned.1.call-update
  204.8 0.9 copy-done.4
  205.6 1.0 convert_reduce_fusion
  206.6 19.4 %psum.7 = s32[1]{0:T(128)} all-reduce(s32[1]{0:T(128)} %bitcast.8), channel_id=1, replica_groups=mesh['dp'=32,'section'=8] {'dp'}, use_global_device_ids=true, to_apply=%region_2.3 | all-reduce | flops 1 | bytes 8 | tf_op jit(solution)/shard_map/psum | solution.py:217
  226.0 79.3 %reduce-scatter.2.cloned.1.call-done = bf16[64,2048]{1,0:T(8,128)(2,1)} async-done(((bf16[2048,2048]{1,0:T(8,128)(2,1)}), bf16[64,2048]{1,0:T(8,128)(2,1)}) %reduce-scatter.2.cloned.1.call-update) | async-done | bytes 262160 | tf_op jit(solution)/shard_map/reduce_scatter | solution.py:224
  305.3 0.0 copy-done.3
  305.3 1.9 add_bitcast_fusion
  (1 shorter events, 0.0 us)
Async XLA Ops:
  7.2 69.4 %copy-start.2 = (f32[1,2048]{1,0:T(1,128)S(1)}, f32[1,2048]{1,0:T(1,128)}, u32[]{:S(2)}) copy-start(f32[1,2048]{1,0:T(1,128)} %gain_ref.1) | copy-start | bytes 24580
  7.2 69.4 %copy-start.1 = (bf16[4,64,2048]{2,1,0:T(8,128)(2,1)S(1)}, bf16[4,64,2048]{2,1,0:T(8,128)(2,1)}, u32[]{:S(2)}) copy-start(bf16[4,64,2048]{2,1,0:T(8,128)(2,1)} %param.7) | copy-start | bytes 3145732
  7.2 69.4 %copy-start = (bf16[4,64,2048]{2,1,0:T(8,128)(2,1)S(1)}, bf16[4,64,2048]{2,1,0:T(8,128)(2,1)}, u32[]{:S(2)}) copy-start(bf16[4,64,2048]{2,1,0:T(8,128)(2,1)} %param.6) | copy-start | bytes 3145732
  7.2 69.4 %all-gather.2.cloned.1.call-start = ((), (), s32[]{:S(2)}) async-start(), calls=%async_computation.1 | async-start | bytes 8650752 | tf_op jit(solution)/shard_map/all_gather | solution.py:219
  14.4 290.9 %reduce-scatter.2.cloned.1.call-start = ((), (), s32[]{:S(2)}) async-start(), calls=%async_computation.2 | async-start | bytes 8650752 | tf_op jit(solution)/shard_map/reduce_scatter | solution.py:224
  204.7 0.9 copy-start.4
  204.7 100.6 %copy-start.3 = (bf16[1,64,2048]{2,1,0:T(8,128)(2,1)S(1)}, bf16[1,64,2048]{2,1,0:T(8,128)(2,1)}, u32[]{:S(2)}) copy-start(bf16[1,64,2048]{2,1,0:T(8,128)(2,1)} %param.8) | copy-start | bytes 786436
Sparse Core Ops, SparseCore 0:
  14.6 61.9 all-gather.1
  204.9 100.3 reduce-scatter.1

commit v2 on v1

v2 whole, which is shorter than its diff:
```python
import functools
import math

import jax
import jax.numpy as jnp
from jax import lax
from jax.experimental import pallas as pl
from jax.experimental.pallas import tpu as pltpu
from jax.sharding import PartitionSpec as P

MESH = pl.DeviceIdType.MESH
epsilon = 1e-06
decay_rate = 4.0
half_root = 0.7071067811865476
density_scale = 0.3989422804014327
BF = jnp.bfloat16
F32 = jnp.float32
SIDE = 4
BLOCKS = SIDE * SIDE


def kernel(micros, sections, token_total, x_hbm, ct_hbm, weight_ref, gain_ref, pair_hbm, earlier_ref, out_ref, flip_ref,
           w, packed, pair, wide_rows, decay, hin, gin, hout, gout, preact, slope, scale, mine, theirs, grad_pre,
           part, part_a, part_b, row_sum, row_a, row_b, flips,
           local_sem, ag_send, ag_recv, mate_recv, f_send, f_recv, b_send, b_recv, mate_n, mate_g, mate_send,
           a_recv, ab_recv, ra_recv, rb_recv, rs_send, flip_send, flip_recv):
    s = lax.axis_index("section")
    dp = lax.axis_index("dp")
    core, xx, yy = dp % 2, (dp // 2) % SIDE, dp // (2 * SIDE)
    last = sections - 1
    rows_all, width = hin.shape
    rows = rows_all // micros
    chunk = 512
    chunks = width // chunk
    shard = weight_ref.shape[0]
    groups = shard // 4
    half_width = width // 2

    def chip(plane, r1, r2):
        dx, dy = jnp.where(plane == 0, r1, r2), jnp.where(plane == 0, r2, r1)
        return ((yy + dy) % SIDE) * SIDE + (xx + dx) % SIDE

    mate = 2 * (dp // 2) + (1 - core)
    right1, left1 = 2 * chip(core, 1, 0) + core, 2 * chip(core, 3, 0) + core
    right2, left2 = 2 * chip(core, 0, 1) + core, 2 * chip(core, 0, 3) + core
    around = (right1, left1, right2, left2)

    def remote(src, dst, send, recv, target):
        return pltpu.make_async_remote_copy(
            src_ref=src, dst_ref=dst, send_sem=send, recv_sem=recv, device_id={"dp": target}, device_id_type=MESH)

    pair_copy = pltpu.make_async_copy(pair_hbm, pair, local_sem.at[0])
    pair_copy.start()
    x_copy = pltpu.make_async_copy(x_hbm, hin, local_sem.at[1])
    ct_copy = pltpu.make_async_copy(ct_hbm, gin, local_sem.at[2])

    @pl.when(s == 0)
    def _():
        x_copy.start()

    @pl.when(s == last)
    def _():
        ct_copy.start()

    barrier = pltpu.get_barrier_semaphore()
    for target in (*around, mate):
        pl.semaphore_signal(barrier, inc=1, device_id={"dp": target}, device_id_type=MESH)

    @pl.when(s > 0)
    def _():
        pl.semaphore_signal(barrier, inc=1, device_id={"section": s - 1}, device_id_type=MESH)

    @pl.when(s < last)
    def _():
        pl.semaphore_signal(barrier, inc=1, device_id={"section": s + 1}, device_id_type=MESH)

    pair_copy.wait()
    own_groups = pl.ds(pl.multiple_of(dp * groups, groups), groups)
    piece = 128
    counted = jnp.zeros((8, 128), jnp.int32)
    for k in range(width // piece):
        cols = pl.ds(k * piece, piece)
        p = pair[own_groups, cols]
        wide_rows[k] = weight_ref[:, cols].astype(F32)
        w0, w1, w2, w3 = (wide_rows[k, pl.ds(j, groups, stride=4), :] for j in range(4))
        lead = jnp.where(p < 3, w0, jnp.where(p == 5, w2, w1))
        trail = jnp.where(p == 0, w1, jnp.where((p == 1) | (p == 3), w2, w3))
        packed[dp, 0:groups, cols] = lead.astype(BF)
        packed[dp, groups:2 * groups, cols] = trail.astype(BF)
        kept = (p < 3, (p == 0) | (p == 3) | (p == 4), (p == 1) | (p == 3) | (p == 5), (p == 2) | (p > 3))
        for j, (k_j, w_j) in enumerate(zip(kept, (w0, w1, w2, w3))):
            decay[k, pl.ds(j, groups, stride=4), :] = jnp.where(k_j, 0.0, decay_rate * w_j)
        e = earlier_ref[:, cols]
        changed = jnp.where(p == e, 0, jnp.where(p + e == 5, 4, 2))
        for a in range(groups // 8):
            for b in range(piece // 128):
                counted = counted + changed[8 * a:8 * a + 8, 128 * b:128 * b + 128]
    flips[0] = counted

    pl.semaphore_wait(barrier, 5 + jnp.where(s > 0, 1, 0) + jnp.where(s < last, 1, 0))

    def send_half(b, h, d):
        at = pl.ds(h * groups, groups)
        remote(packed.at[2 * b + core, at], packed.at[2 * b + core, at], ag_send.at[d], ag_recv.at[b, h],
               around[d]).start()

    def send_mate(b):
        remote(packed.at[2 * b + core], packed.at[2 * b + core], ag_send.at[4], mate_recv.at[b], mate).start()

    def wait_half(b, h):
        at = pl.ds(h * groups, groups)
        remote(packed.at[2 * b + core, at], packed.at[2 * b + core, at], ag_send.at[0], ag_recv.at[b, h],
               mate).wait_recv()

    def wait_mate(b):
        slot = 2 * b + (1 - core)
        remote(packed.at[slot], packed.at[slot], ag_send.at[4], mate_recv.at[b], mate).wait_recv()

    def spread(b):
        for d in (2, 3):
            send_half(b, 0, d)
            send_half(b, 1, d)
        send_mate(b)

    def unpack(slot):
        at = pl.ds(pl.multiple_of(slot * groups, groups), groups)
        to = pl.ds(pl.multiple_of(slot * shard, shard), shard)
        for k in range(width // piece):
            cols = pl.ds(k * piece, piece)
            p = pair[at, cols]
            lead = packed[slot, 0:groups, cols].astype(F32)
            trail = packed[slot, groups:2 * groups, cols].astype(F32)
            o0 = jnp.where(p < 3, lead, 0.0)
            o1 = jnp.where(p == 0, trail, jnp.where((p == 3) | (p == 4), lead, 0.0))
            o2 = jnp.where(p == 5, lead, jnp.where((p == 1) | (p == 3), trail, 0.0))
            o3 = jnp.where((p == 2) | (p > 3), trail, 0.0)
            for j, o in enumerate((o0, o1, o2, o3)):
                wide_rows[k, pl.ds(j, groups, stride=4), :] = o
            w[to, cols] = wide_rows[k].astype(BF)

    def flip_copy(src, dst, target):
        return remote(flips.at[src], flips.at[dst], flip_send.at[dst - 1], flip_recv.at[dst - 1], target)

    own = chip(core, 0, 0)
    for d in (0, 1):
        send_half(own, 0, d)
        send_half(own, 1, d)
    spread(own)
    flip_copy(0, 1, mate).start()
    unpack(dp)
    from_left, from_right, far = chip(core, 3, 0), chip(core, 1, 0), chip(core, 2, 0)
    wait_half(from_left, 0)
    send_half(from_left, 0, 0)
    wait_half(from_left, 1)
    spread(from_left)
    wait_half(from_right, 1)
    send_half(from_right, 1, 1)
    wait_half(from_right, 0)
    spread(from_right)
    flip_copy(0, 1, mate).wait_recv()
    flips[8] = flips[0] + flips[1]
    flip_copy(8, 2, right1).start()
    flip_copy(8, 3, left1).start()
    unpack(2 * from_left + core)
    wait_half(far, 0)
    wait_half(far, 1)
    spread(far)

    def near(i, carry):
        r1 = jnp.where(i == 0, 0, jnp.where(i == 1, 3, jnp.where(i == 2, 1, 2)))
        lower, upper = chip(core, r1, 3), chip(core, r1, 1)
        wait_half(lower, 0)
        send_half(lower, 0, 2)
        wait_half(lower, 1)
        send_mate(lower)
        wait_half(upper, 1)
        send_half(upper, 1, 3)
        wait_half(upper, 0)
        send_mate(upper)
        other = chip(1 - core, r1, 0)
        wait_mate(other)

        def expand(j, c):
            unpack(jnp.where(j == 0, 2 * other + (1 - core), jnp.where(j == 1, 2 * lower + core, 2 * upper + core)))
            return c

        lax.fori_loop(0, 3, expand, 0)
        return carry

    lax.fori_loop(0, SIDE, near, 0)

    def expand_rest(j, c):
        unpack(2 * jnp.where(j == 0, from_right, far) + core)
        return c

    lax.fori_loop(0, 2, expand_rest, 0)
    flip_copy(8, 2, right1).wait_recv()
    flip_copy(2, 4, right1).start()

    def distant(i, carry):
        r1 = jnp.where(i == 0, 0, jnp.where(i == 1, 3, jnp.where(i == 2, 1, 2)))
        beyond = chip(core, r1, 2)
        wait_half(beyond, 0)
        wait_half(beyond, 1)
        send_mate(beyond)
        lower, upper = chip(1 - core, r1, 3), chip(1 - core, r1, 1)
        wait_mate(lower)
        wait_mate(upper)

        def expand(j, c):
            unpack(jnp.where(j == 0, 2 * beyond + core,
                             jnp.where(j == 1, 2 * lower + (1 - core), 2 * upper + (1 - core))))
            return c

        lax.fori_loop(0, 3, expand, 0)
        return carry

    lax.fori_loop(0, SIDE, distant, 0)

    def final(i, carry):
        r1 = jnp.where(i == 0, 0, jnp.where(i == 1, 3, jnp.where(i == 2, 1, 2)))
        b = chip(1 - core, r1, 2)
        wait_mate(b)
        unpack(2 * b + (1 - core))
        return carry

    lax.fori_loop(0, SIDE, final, 0)

    flip_copy(8, 3, left1).wait_recv()
    flip_copy(2, 4, right1).wait_recv()
    flips[9] = flips[8] + flips[2] + flips[3] + flips[4]
    flip_copy(9, 5, right2).start()
    flip_copy(9, 6, left2).start()

    @pl.when(s == 0)
    def _():
        x_copy.wait()

    @pl.when(s == last)
    def _():
        ct_copy.wait()

    def z_copy(src, dst, send, recv, where, target):
        return pltpu.make_async_remote_copy(
            src_ref=src.at[where], dst_ref=dst.at[where], send_sem=send, recv_sem=recv,
            device_id={"section": target}, device_id_type=MESH)

    def forward_copy(m, where):
        return z_copy(hout, hin, f_send.at[m], f_recv.at[m], where, jnp.minimum(s + 1, last))

    def backward_copy(m, where):
        return z_copy(gout, gin, b_send.at[m], b_recv.at[m], where, jnp.maximum(s - 1, 0))

    def mate_copy(src, dst, sems, k, m):
        at = pl.ds(pl.multiple_of(m * rows, rows), rows)
        to = pl.ds(pl.multiple_of(rows_all + m * rows, rows), rows)
        return remote(src.at[at], dst.at[to], mate_send.at[k, m], sems.at[m], mate)

    def forward(m, carry):
        at = pl.ds(pl.multiple_of(m * rows, rows), rows)

        @pl.when(s > 0)
        def _():
            forward_copy(m, (at,)).wait_recv()

        values = hin[at, :].astype(F32)
        q = lax.rsqrt(jnp.sum(values * values, axis=-1, keepdims=True) * (1.0 / width) + epsilon)
        scale[at, :] = jnp.broadcast_to(q, (rows, 128))
        normal = (values * q * gain_ref[...]).astype(BF)
        for c in range(chunks):
            cols = pl.ds(c * chunk, chunk)
            p = jnp.dot(normal, w[:, cols], preferred_element_type=F32)
            cdf = 0.5 * (1.0 + lax.erf(p * half_root))
            hout[at, cols] = (hin[at, cols].astype(F32) + p * cdf).astype(BF)

            @pl.when(s < last)
            def _():
                forward_copy(m, (at, cols)).start()

            preact[at, cols] = p
            slope[at, cols] = cdf + p * (jnp.exp(-0.5 * p * p) * density_scale)
        low = lax.broadcasted_iota(jnp.int32, (rows, 128), 1) < 64
        for k in range(width // 256):
            first = hin[at, pl.ds(256 * k, 128)].astype(F32) * q * gain_ref[:, pl.ds(256 * k, 128)]
            second = hin[at, pl.ds(256 * k + 128, 128)].astype(F32) * q * gain_ref[:, pl.ds(256 * k + 128, 128)]
            even = jnp.where(low, first, pltpu.roll(second, 64, 1))
            odd = jnp.where(low, pltpu.roll(first, 64, 1), second)
            cols = pl.ds(128 * k, 128)
            mine[at, cols] = jnp.where(core == 0, even, odd).astype(BF)
            theirs[at, cols] = jnp.where(core == 0, odd, even).astype(BF)
        mate_copy(theirs, mine, mate_n, 0, m).start()
        return carry

    lax.fori_loop(0, micros, forward, 0)

    flip_copy(9, 5, right2).wait_recv()
    flip_copy(5, 7, right2).start()

    def backward(m, carry):
        at = pl.ds(pl.multiple_of(m * rows, rows), rows)

        @pl.when(s < last)
        def _():
            backward_copy(m, (at,)).wait_recv()

        gp = (gin[at, :].astype(F32) * slope[at, :]).astype(BF)
        grad_pre[at, :] = gp
        mate_copy(grad_pre, grad_pre, mate_g, 1, m).start()

        @pl.when(s > 0)
        def _():
            q = scale[at, 0:1]
            mean = jnp.sum(gp.astype(F32) * preact[at, :], axis=-1, keepdims=True) * (1.0 / width)
            pull = q * q * mean
            for c in range(chunks):
                cols = pl.ds(c * chunk, chunk)
                a = lax.dot_general(gp, w[cols, :], (((1,), (1,)), ((), ())), preferred_element_type=F32)
                a = a * gain_ref[:, cols]
                gout[at, cols] = (gin[at, cols].astype(F32) + q * a - hin[at, cols].astype(F32) * pull).astype(BF)
                backward_copy(m, (at, cols)).start()
        return carry

    lax.fori_loop(0, micros, backward, 0)

    def mate_rows(m, carry):
        mate_copy(theirs, mine, mate_n, 0, m).wait_recv()
        mate_copy(grad_pre, grad_pre, mate_g, 1, m).wait_recv()
        return carry

    lax.fori_loop(0, micros, mate_rows, 0)

    def terms(i, carry):
        cols = pl.ds(pl.multiple_of(i * 256, 256), 256)
        part[cols, :] = lax.dot_general(
            mine[:, cols], grad_pre[...], (((0,), (0,)), ((), ())), preferred_element_type=F32).astype(BF)
        return carry

    lax.fori_loop(0, half_width // 256, terms, 0)

    def block(r1, r2):
        return pl.ds(pl.multiple_of(chip(core, r1, r2) * shard, shard), shard)

    def slot(r2, count=1):
        return pl.ds(r2 * shard, count * shard)

    def first_ring(src_r1, r2, d, dst, dst_slot, recv):
        return remote(part.at[block(src_r1, r2)], dst.at[dst_slot], rs_send.at[d], recv, around[d])

    toward_left, toward_right = (2, 1), (3, 0)
    for r2 in toward_left:
        first_ring(2, r2, 1, part_a, slot(r2), a_recv.at[r2]).start()
    for r2 in toward_right:
        first_ring(2, r2, 0, part_a, slot(r2), a_recv.at[r2]).start()
    for r2 in toward_right:
        first_ring(3, r2, 1, part_b, slot(r2), ab_recv.at[0, r2]).start()
    for r2 in toward_left:
        first_ring(1, r2, 0, part_b, slot(4 + r2), ab_recv.at[1, r2]).start()
    for k in range(2):
        for r2, r1, d, side in ((toward_left[k], 3, 1, 0), (toward_right[k], 1, 0, 1)):
            first_ring(2, r2, d, part_a, slot(r2), a_recv.at[r2]).wait_recv()
            at = block(r1, r2)
            part[at, :] = (part[at, :].astype(F32) + part_a[slot(r2), :].astype(F32)).astype(BF)
            first_ring(r1, r2, d, part_b, slot(4 * side + r2), ab_recv.at[side, r2]).start()

    flip_copy(9, 6, left2).wait_recv()
    flip_copy(5, 7, right2).wait_recv()
    all_flips = flips[9] + flips[5] + flips[6] + flips[7]
    flip_ref[0] = jnp.sum(all_flips.astype(F32)).astype(jnp.int32)

    def ring_total(r2):
        for side in range(2):
            first_ring(3, r2, 1, part_b, slot(4 * side + r2), ab_recv.at[side, r2]).wait_recv()
        total = part[block(0, r2), :].astype(F32) + part_b[slot(r2), :].astype(F32) + part_b[slot(4 + r2), :].astype(F32)
        row_sum[slot(r2), :] = total.astype(BF)

    half = shard // 2

    def second_ring(r2, h, d, dst, start, recv):
        return remote(row_sum.at[pl.ds(r2 * shard + h * half, half)], dst.at[pl.ds(start, half)], rs_send.at[d], recv,
                      around[d])

    ring_total(2)
    second_ring(2, 0, 3, row_a, 0, ra_recv.at[0]).start()
    second_ring(2, 1, 2, row_a, half, ra_recv.at[1]).start()
    ring_total(3)
    second_ring(3, 1, 3, row_b, half, rb_recv.at[0, 1]).start()
    ring_total(1)
    second_ring(1, 0, 2, row_b, shard, rb_recv.at[1, 0]).start()
    for h, r2, d, side in ((0, 3, 3, 0), (1, 1, 2, 1)):
        second_ring(2, h, d, row_a, h * half, ra_recv.at[h]).wait_recv()
        at = pl.ds(r2 * shard + h * half, half)
        row_sum[at, :] = (row_sum[at, :].astype(F32) + row_a[pl.ds(h * half, half), :].astype(F32)).astype(BF)
        second_ring(r2, h, d, row_b, side * shard + h * half, rb_recv.at[side, h]).start()
    ring_total(0)
    for side, h in ((0, 1), (1, 0), (0, 0), (1, 1)):
        second_ring(2, h, 3, row_b, side * shard + h * half, rb_recv.at[side, h]).wait_recv()
    for k in range(width // piece):
        cols = pl.ds(k * piece, piece)
        total = row_sum[slot(0), cols].astype(F32) + row_b[slot(0), cols].astype(F32) + row_b[slot(1), cols].astype(F32)
        out_ref[:, cols] = total * (1.0 / math.sqrt(token_total)) + decay[k]

    def drain(m, carry):
        at = pl.ds(pl.multiple_of(m * rows, rows), rows)

        @pl.when(s < last)
        def _():
            forward_copy(m, (at,)).wait_send()

        @pl.when(s > 0)
        def _():
            backward_copy(m, (at,)).wait_send()

        mate_copy(theirs, mine, mate_n, 0, m).wait_send()
        mate_copy(grad_pre, grad_pre, mate_g, 1, m).wait_send()
        return carry

    lax.fori_loop(0, micros, drain, 0)

    def sent(sem, count):
        ref = grad_pre.at[pl.ds(0, count)]
        remote(ref, ref, sem, flip_recv.at[0], mate).wait_send()

    for d in (0, 1):
        sent(ag_send.at[d], 3 * groups)
    for d in (2, 3):
        sent(ag_send.at[d], 12 * groups)
    sent(ag_send.at[4], 2 * BLOCKS * groups)
    for d in (0, 1):
        sent(rs_send.at[d], 6 * shard)
    for d in (2, 3):
        sent(rs_send.at[d], 3 * half)
    for dst in range(1, 8):
        flip_copy(0, dst, mate).wait_send()


def step(x, ct, weight, gain, pair, earlier, sections, token_total, micros):
    rows, width = x.shape
    shard = weight.shape[0]
    groups = shard // 4
    vmem = pl.BlockSpec(memory_space=pltpu.VMEM)
    hbm = pl.BlockSpec(memory_space=pl.ANY)
    act = pltpu.VMEM((rows, width), BF)
    wide = pltpu.VMEM((rows, width), F32)
    dma = pltpu.SemaphoreType.DMA
    return pl.pallas_call(
        functools.partial(kernel, micros, sections, token_total),
        out_shape=(jax.ShapeDtypeStruct((shard, width), F32), jax.ShapeDtypeStruct((1,), jnp.int32)),
        in_specs=[hbm, hbm, vmem, vmem, hbm, vmem],
        out_specs=(vmem, pl.BlockSpec(memory_space=pltpu.SMEM)),
        scratch_shapes=[
            pltpu.VMEM((width, width), BF),
            pltpu.VMEM((2 * BLOCKS, 2 * groups, width), BF),
            pltpu.VMEM(pair.shape, jnp.int32),
            pltpu.VMEM((width // 128, shard, 128), F32),
            pltpu.VMEM((width // 128, shard, 128), F32),
            act, act, act, act, wide, wide, pltpu.VMEM((rows, 128), F32),
            pltpu.VMEM((2 * rows, width // 2), BF),
            pltpu.VMEM((rows, width // 2), BF),
            pltpu.VMEM((2 * rows, width), BF),
            pltpu.VMEM((width // 2, width), BF),
            pltpu.VMEM((SIDE * shard, width), BF),
            pltpu.VMEM((2 * SIDE * shard, width), BF),
            pltpu.VMEM((SIDE * shard, width), BF),
            pltpu.VMEM((shard, width), BF),
            pltpu.VMEM((2 * shard, width), BF),
            pltpu.VMEM((10, 8, 128), jnp.int32),
            dma((3,)), dma((5,)), dma((BLOCKS, 2)), dma((BLOCKS,)),
            dma((micros,)), dma((micros,)), dma((micros,)), dma((micros,)),
            dma((micros,)), dma((micros,)), dma((2, micros)),
            dma((SIDE,)), dma((2, SIDE)), dma((2,)), dma((2, 2)), dma((4,)), dma((7,)), dma((7,)),
        ],
        compiler_params=pltpu.CompilerParams(
            collective_id=0, has_side_effects=True, vmem_limit_bytes=56 * 1024 * 1024),
    )(x, ct, weight, gain, pair, earlier)


def body(activations, cotangent, weight, norm_gain, pair_mask, earlier_mask):
    micro_count, row_count, model_width = activations.shape
    tokens = micro_count * row_count
    gradient, flip_sum = step(
        activations.reshape(tokens, model_width), cotangent.reshape(tokens, model_width), weight[0], norm_gain,
        pair_mask[0], earlier_mask[0], lax.axis_size("section"), tokens * lax.axis_size("dp"), 8)
    return (gradient[None], flip_sum)


def solution(mesh):
    placed = (
        P(None, "dp", None),
        P(None, "dp", None),
        P("section", "dp", None),
        P("section", None),
        P("section", None, None),
        P("section", "dp", None),
    )
    return jax.shard_map(
        body,
        mesh=mesh,
        in_specs=placed,
        out_specs=(P("section", "dp", None), P("section")),
        check_vma=False,
    )
```

time: 315 us -> 186 us (0.59)
  waiting for transfers between devices: 141 us -> 0 us
  Pallas kernels: 128 us -> 181 us
  blocking collectives: 19.4 us -> 0 us
  between operations: 14.1 us -> 2.34 us
  other arithmetic: 8.5 us -> 0 us
    reduce_scatter x1 -> x0, waiting for transfers between devices: 79.3 us -> none  [body(): lax.psum_scatter(partial, 'dp', scatter_dimension=0, tiled=True)]
    all_gather x1 -> x0, waiting for transfers between devices: 62.1 us -> none  [body(): masked = lax.all_gather(masked_shard, 'dp', axis=0, tiled=True)]
    pallas_call x1, Pallas kernels: 128 us -> 181 us  [step(): pl.pallas_call(functools.partial(kernel, micros, sections, token_total),...]
    psum x1 -> x0, blocking collectives: 19.4 us -> none  [body(): flip_sum = lax.psum(flip_local, 'dp')]
    select_n x3 -> x0, other arithmetic: 5.64 us -> none  [the longest x2 3.53 us: pair_ends(): leading = jnp.where(matches, first_table[pair_index], leading)]
  transfers between devices with their start and end apart: 2 -> 0, of which waited for: 2 -> 0; matrix products, arithmetic and copies ran while one was open for 0% -> 0% of each run, Pallas kernels for 0% -> 0%
where the time goes in v2:
time: 186 us
  Pallas kernels  181 us (97%)
  between operations  2.34 us (1%)
  local copies, waits for them, and re-layouts  1.87 us (1%)
    pallas_call x1, Pallas kernels, step(): pl.pallas_call(functools.partial(kernel, micros, sections, token_total),...  181 us

profile of v2, /device:TPU:1, one launch (start us, length us, event | category | flops | bytes accessed | tf_op | source)
XLA Modules:
  0.0 185.6 jit_solution(4434754230050886189)
XLA Ops:
  0.6 181.4 %shard_map.77 = (f32[64,2048]{1,0:T(8,128)}, s32[1]{0:T(128)}) custom-call(bf16[256,2048]{1,0:T(8,128)(2,1)} %bitcast.7, bf16[256,2048]{1,0:T(8,128)(2,1)} %bitcast.8, bf16[64,2048]{1,0:T(8,128)(2,1)} %bitcast.10, f32[1,2048]{1,0:T(1,128)} %gain_ref.1, s32[512,2048]{1,0:T(8,128)} %bitcast.6, s32[16,2048]{1,0:T(8,128)} %bitcast.11), custom_call_target="tpu_custom_call" | custom-call | tf_op jit(solution)/shard_map/pallas_call | solution.py:445
  182.0 1.9 %copy.10 = f32[1,64,2048]{2,1,0:T(8,128)} copy(f32[1,64,2048]{2,1,0:T(8,128)} %bitcast.9) | data formatting | bytes 1048576

commit v3 on v2

--- a/solution.py
+++ b/solution.py
@@ -20,16 +20,18 @@
 
 
 def kernel(micros, sections, token_total, x_hbm, ct_hbm, weight_ref, gain_ref, pair_hbm, earlier_ref, out_ref, flip_ref,
-           w, packed, pair, wide_rows, decay, hin, gin, hout, gout, preact, slope, scale, mine, theirs, grad_pre,
-           part, part_a, part_b, row_sum, row_a, row_b, flips,
-           local_sem, ag_send, ag_recv, mate_recv, f_send, f_recv, b_send, b_recv, mate_n, mate_g, mate_send,
+           w, turned, packed, pair, wide_rows, decay, arriving, leaving, hidden, preact, slope, scale, mine, theirs,
+           grad_pre, part, part_a, part_b, row_sum, row_a, row_b, flips,
+           local_sem, ag_send, ag_recv, mate_recv, in_send, in_recv, z_send, z_recv, mate_n, mate_g, mate_f, mate_send,
            a_recv, ab_recv, ra_recv, rb_recv, rs_send, flip_send, flip_recv):
     s = lax.axis_index("section")
     dp = lax.axis_index("dp")
     core, xx, yy = dp % 2, (dp // 2) % SIDE, dp // (2 * SIDE)
     last = sections - 1
-    rows_all, width = hin.shape
+    rows_all, width = arriving.shape
     rows = rows_all // micros
+    half_rows = rows_all // 2
+    forward_core, backward_core = core == 1, core == 0
     chunk = 512
     chunks = width // chunk
     shard = weight_ref.shape[0]
@@ -51,14 +53,16 @@
 
     pair_copy = pltpu.make_async_copy(pair_hbm, pair, local_sem.at[0])
     pair_copy.start()
-    x_copy = pltpu.make_async_copy(x_hbm, hin, local_sem.at[1])
-    ct_copy = pltpu.make_async_copy(ct_hbm, gin, local_sem.at[2])
-
-    @pl.when(s == 0)
+    x_copy = pltpu.make_async_copy(x_hbm, arriving.at[pl.ds(0, half_rows)], local_sem.at[1])
+    ct_copy = pltpu.make_async_copy(ct_hbm, arriving.at[pl.ds(half_rows, half_rows)], local_sem.at[1])
+    x_mate = remote(x_hbm, arriving.at[pl.ds(half_rows, half_rows)], in_send.at[0], in_recv.at[0], mate)
+    ct_mate = remote(ct_hbm, arriving.at[pl.ds(0, half_rows)], in_send.at[0], in_recv.at[0], mate)
+
+    @pl.when((s == 0) & forward_core)
     def _():
         x_copy.start()
 
-    @pl.when(s == last)
+    @pl.when((s == last) & backward_core)
     def _():
         ct_copy.start()
 
@@ -98,6 +102,14 @@
     flips[0] = counted
 
     pl.semaphore_wait(barrier, 5 + jnp.where(s > 0, 1, 0) + jnp.where(s < last, 1, 0))
+
+    @pl.when((s == 0) & backward_core)
+    def _():
+        x_mate.start()
+
+    @pl.when((s == last) & forward_core)
+    def _():
+        ct_mate.start()
 
     def send_half(b, h, d):
         at = pl.ds(h * groups, groups)
@@ -232,38 +244,40 @@
     flip_copy(9, 5, right2).start()
     flip_copy(9, 6, left2).start()
 
-    @pl.when(s == 0)
-    def _():
-        x_copy.wait()
-
-    @pl.when(s == last)
-    def _():
-        ct_copy.wait()
-
-    def z_copy(src, dst, send, recv, where, target):
+    def tile_rows(m):
+        return pl.ds(pl.multiple_of(m * rows, rows), rows)
+
+    def z_copy(m, where, target):
         return pltpu.make_async_remote_copy(
-            src_ref=src.at[where], dst_ref=dst.at[where], send_sem=send, recv_sem=recv,
+            src_ref=leaving.at[where], dst_ref=arriving.at[where], send_sem=z_send.at[m], recv_sem=z_recv.at[m],
             device_id={"section": target}, device_id_type=MESH)
 
     def forward_copy(m, where):
-        return z_copy(hout, hin, f_send.at[m], f_recv.at[m], where, jnp.minimum(s + 1, last))
+        return z_copy(m, where, jnp.minimum(s + 1, last))
 
     def backward_copy(m, where):
-        return z_copy(gout, gin, b_send.at[m], b_recv.at[m], where, jnp.maximum(s - 1, 0))
-
-    def mate_copy(src, dst, sems, k, m):
-        at = pl.ds(pl.multiple_of(m * rows, rows), rows)
-        to = pl.ds(pl.multiple_of(rows_all + m * rows, rows), rows)
-        return remote(src.at[at], dst.at[to], mate_send.at[k, m], sems.at[m], mate)
+        return z_copy(m, where, jnp.maximum(s - 1, 0))
+
+    def half_copy(m):
+        return remote(theirs.at[tile_rows(m)], mine.at[tile_rows(m)], mate_send.at[0, m], mate_n.at[m], mate)
+
+    def grad_copy(m):
+        return remote(grad_pre.at[tile_rows(m)], grad_pre.at[tile_rows(m)], mate_send.at[0, m], mate_g.at[m], mate)
+
+    def saved_copy(k, m):
+        src = (arriving, slope, preact, scale)[k]
+        dst = (hidden, slope, preact, scale)[k]
+        return remote(src.at[tile_rows(m)], dst.at[tile_rows(m)], mate_send.at[1 + k, m], mate_f.at[k, m], mate)
 
     def forward(m, carry):
-        at = pl.ds(pl.multiple_of(m * rows, rows), rows)
+        at = tile_rows(m)
 
         @pl.when(s > 0)
         def _():
             forward_copy(m, (at,)).wait_recv()
 
-        values = hin[at, :].astype(F32)
+        saved_copy(0, m).start()
+        values = arriving[at, :].astype(F32)
         q = lax.rsqrt(jnp.sum(values * values, axis=-1, keepdims=True) * (1.0 / width) + epsilon)
         scale[at, :] = jnp.broadcast_to(q, (rows, 128))
         normal = (values * q * gain_ref[...]).astype(BF)
@@ -271,63 +285,89 @@
             cols = pl.ds(c * chunk, chunk)
             p = jnp.dot(normal, w[:, cols], preferred_element_type=F32)
             cdf = 0.5 * (1.0 + lax.erf(p * half_root))
-            hout[at, cols] = (hin[at, cols].astype(F32) + p * cdf).astype(BF)
+            leaving[at, cols] = (arriving[at, cols].astype(F32) + p * cdf).astype(BF)
 
             @pl.when(s < last)
             def _():
                 forward_copy(m, (at, cols)).start()
 
-            preact[at, cols] = p
-            slope[at, cols] = cdf + p * (jnp.exp(-0.5 * p * p) * density_scale)
+            preact[at, cols] = p.astype(BF)
+            slope[at, cols] = (cdf + p * (jnp.exp(-0.5 * p * p) * density_scale)).astype(BF)
+        for k in (1, 2, 3):
+            saved_copy(k, m).start()
         low = lax.broadcasted_iota(jnp.int32, (rows, 128), 1) < 64
         for k in range(width // 256):
-            first = hin[at, pl.ds(256 * k, 128)].astype(F32) * q * gain_ref[:, pl.ds(256 * k, 128)]
-            second = hin[at, pl.ds(256 * k + 128, 128)].astype(F32) * q * gain_ref[:, pl.ds(256 * k + 128, 128)]
-            even = jnp.where(low, first, pltpu.roll(second, 64, 1))
-            odd = jnp.where(low, pltpu.roll(first, 64, 1), second)
+            first = arriving[at, pl.ds(256 * k, 128)].astype(F32) * q * gain_ref[:, pl.ds(256 * k, 128)]
+            second = arriving[at, pl.ds(256 * k + 128, 128)].astype(F32) * q * gain_ref[:, pl.ds(256 * k + 128, 128)]
             cols = pl.ds(128 * k, 128)
-            mine[at, cols] = jnp.where(core == 0, even, odd).astype(BF)
-            theirs[at, cols] = jnp.where(core == 0, odd, even).astype(BF)
-        mate_copy(theirs, mine, mate_n, 0, m).start()
-        return carry
-
-    lax.fori_loop(0, micros, forward, 0)
-
-    flip_copy(9, 5, right2).wait_recv()
-    flip_copy(5, 7, right2).start()
+            theirs[at, cols] = jnp.where(low, first, pltpu.roll(second, 64, 1)).astype(BF)
+            mine[at, cols] = jnp.where(low, pltpu.roll(first, 64, 1), second).astype(BF)
+        half_copy(m).start()
+        return carry
 
     def backward(m, carry):
-        at = pl.ds(pl.multiple_of(m * rows, rows), rows)
+        at = tile_rows(m)
+        for k in (0, 1, 2, 3):
+            saved_copy(k, m).wait_recv()
 
         @pl.when(s < last)
         def _():
             backward_copy(m, (at,)).wait_recv()
 
-        gp = (gin[at, :].astype(F32) * slope[at, :]).astype(BF)
+        gp = (arriving[at, :].astype(F32) * slope[at, :].astype(F32)).astype(BF)
         grad_pre[at, :] = gp
-        mate_copy(grad_pre, grad_pre, mate_g, 1, m).start()
+        grad_copy(m).start()
 
         @pl.when(s > 0)
         def _():
             q = scale[at, 0:1]
-            mean = jnp.sum(gp.astype(F32) * preact[at, :], axis=-1, keepdims=True) * (1.0 / width)
+            mean = jnp.sum(gp.astype(F32) * preact[at, :].astype(F32), axis=-1, keepdims=True) * (1.0 / width)
             pull = q * q * mean
             for c in range(chunks):
                 cols = pl.ds(c * chunk, chunk)
-                a = lax.dot_general(gp, w[cols, :], (((1,), (1,)), ((), ())), preferred_element_type=F32)
+                a = jnp.dot(gp, turned[:, cols], preferred_element_type=F32)
                 a = a * gain_ref[:, cols]
-                gout[at, cols] = (gin[at, cols].astype(F32) + q * a - hin[at, cols].astype(F32) * pull).astype(BF)
+                leaving[at, cols] = (arriving[at, cols].astype(F32) + q * a - hidden[at, cols].astype(F32) * pull).astype(BF)
                 backward_copy(m, (at, cols)).start()
         return carry
 
-    lax.fori_loop(0, micros, backward, 0)
-
-    def mate_rows(m, carry):
-        mate_copy(theirs, mine, mate_n, 0, m).wait_recv()
-        mate_copy(grad_pre, grad_pre, mate_g, 1, m).wait_recv()
-        return carry
-
-    lax.fori_loop(0, micros, mate_rows, 0)
+    def received_grad(m, carry):
+        grad_copy(m).wait_recv()
+        return carry
+
+    def received_half(m, carry):
+        half_copy(m).wait_recv()
+        return carry
+
+    @pl.when(forward_core)
+    def _():
+        @pl.when(s == 0)
+        def _():
+            x_copy.wait()
+            x_mate.wait_recv()
+
+        lax.fori_loop(0, micros, forward, 0)
+        lax.fori_loop(0, micros, received_grad, 0)
+
+    @pl.when(backward_core)
+    def _():
+        def turn(i, carry):
+            at = pl.ds(pl.multiple_of(i * 128, 128), 128)
+            turned[:, at] = w[at, :].T
+            return carry
+
+        lax.fori_loop(0, width // 128, turn, 0)
+
+        @pl.when(s == last)
+        def _():
+            ct_copy.wait()
+            ct_mate.wait_recv()
+
+        lax.fori_loop(0, micros, backward, 0)
+        lax.fori_loop(0, micros, received_half, 0)
+
+    flip_copy(9, 5, right2).wait_recv()
+    flip_copy(5, 7, right2).start()
 
     def terms(i, carry):
         cols = pl.ds(pl.multiple_of(i * 256, 256), 256)
@@ -399,22 +439,39 @@
         total = row_sum[slot(0), cols].astype(F32) + row_b[slot(0), cols].astype(F32) + row_b[slot(1), cols].astype(F32)
         out_ref[:, cols] = total * (1.0 / math.sqrt(token_total)) + decay[k]
 
-    def drain(m, carry):
-        at = pl.ds(pl.multiple_of(m * rows, rows), rows)
-
+    def drain_forward(m, carry):
         @pl.when(s < last)
         def _():
-            forward_copy(m, (at,)).wait_send()
-
+            forward_copy(m, (tile_rows(m),)).wait_send()
+
+        half_copy(m).wait_send()
+        for k in range(4):
+            saved_copy(k, m).wait_send()
+        return carry
+
+    def drain_backward(m, carry):
         @pl.when(s > 0)
         def _():
-            backward_copy(m, (at,)).wait_send()
-
-        mate_copy(theirs, mine, mate_n, 0, m).wait_send()
-        mate_copy(grad_pre, grad_pre, mate_g, 1, m).wait_send()
-        return carry
-
-    lax.fori_loop(0, micros, drain, 0)
+            backward_copy(m, (tile_rows(m),)).wait_send()
+
+        grad_copy(m).wait_send()
+        return carry
+
+    @pl.when(forward_core)
+    def _():
+        lax.fori_loop(0, micros, drain_forward, 0)
+
+        @pl.when(s == last)
+        def _():
+            ct_mate.wait_send()
+
+    @pl.when(backward_core)
+    def _():
+        lax.fori_loop(0, micros, drain_backward, 0)
+
+        @pl.when(s == 0)
+        def _():
+            x_mate.wait_send()
 
     def sent(sem, count):
         ref = grad_pre.at[pl.ds(0, count)]
@@ -439,8 +496,7 @@
     groups = shard // 4
     vmem = pl.BlockSpec(memory_space=pltpu.VMEM)
     hbm = pl.BlockSpec(memory_space=pl.ANY)
-    act = pltpu.VMEM((rows, width), BF)
-    wide = pltpu.VMEM((rows, width), F32)
+    act = pltpu.VMEM((2 * rows, width), BF)
     dma = pltpu.SemaphoreType.DMA
     return pl.pallas_call(
         functools.partial(kernel, micros, sections, token_total),
@@ -449,13 +505,14 @@
         out_specs=(vmem, pl.BlockSpec(memory_space=pltpu.SMEM)),
         scratch_shapes=[
             pltpu.VMEM((width, width), BF),
+            pltpu.VMEM((width, width), BF),
             pltpu.VMEM((2 * BLOCKS, 2 * groups, width), BF),
             pltpu.VMEM(pair.shape, jnp.int32),
             pltpu.VMEM((width // 128, shard, 128), F32),
             pltpu.VMEM((width // 128, shard, 128), F32),
-            act, act, act, act, wide, wide, pltpu.VMEM((rows, 128), F32),
+            act, act, act, act, act, pltpu.VMEM((2 * rows, 128), F32),
             pltpu.VMEM((2 * rows, width // 2), BF),
-            pltpu.VMEM((rows, width // 2), BF),
+            pltpu.VMEM((2 * rows, width // 2), BF),
             pltpu.VMEM((2 * rows, width), BF),
             pltpu.VMEM((width // 2, width), BF),
             pltpu.VMEM((SIDE * shard, width), BF),
@@ -464,13 +521,12 @@
             pltpu.VMEM((shard, width), BF),
             pltpu.VMEM((2 * shard, width), BF),
             pltpu.VMEM((10, 8, 128), jnp.int32),
-            dma((3,)), dma((5,)), dma((BLOCKS, 2)), dma((BLOCKS,)),
-            dma((micros,)), dma((micros,)), dma((micros,)), dma((micros,)),
-            dma((micros,)), dma((micros,)), dma((2, micros)),
+            dma((2,)), dma((5,)), dma((BLOCKS, 2)), dma((BLOCKS,)), dma((1,)), dma((1,)),
+            dma((micros,)), dma((micros,)), dma((micros,)), dma((micros,)), dma((4, micros)), dma((5, micros)),
             dma((SIDE,)), dma((2, SIDE)), dma((2,)), dma((2, 2)), dma((4,)), dma((7,)), dma((7,)),
         ],
         compiler_params=pltpu.CompilerParams(
-            collective_id=0, has_side_effects=True, vmem_limit_bytes=56 * 1024 * 1024),
+            collective_id=0, has_side_effects=True, vmem_limit_bytes=58 * 1024 * 1024),
     )(x, ct, weight, gain, pair, earlier)
 
 
@@ -479,7 +535,7 @@
     tokens = micro_count * row_count
     gradient, flip_sum = step(
         activations.reshape(tokens, model_width), cotangent.reshape(tokens, model_width), weight[0], norm_gain,
-        pair_mask[0], earlier_mask[0], lax.axis_size("section"), tokens * lax.axis_size("dp"), 8)
+        pair_mask[0], earlier_mask[0], lax.axis_size("section"), tokens * lax.axis_size("dp"), 16)
     return (gradient[None], flip_sum)
 
 

time: 186 us -> 163 us (0.88)
  Pallas kernels: 181 us -> 159 us
    pallas_call x1, Pallas kernels: 181 us -> 159 us  [step(): pl.pallas_call(functools.partial(kernel, micros, sections, token_total),...]
where the time goes in v3:
time: 163 us
  Pallas kernels  159 us (98%)
  between operations  2.34 us (1%)
  local copies, waits for them, and re-layouts  1.87 us (1%)
    pallas_call x1, Pallas kernels, step(): pl.pallas_call(functools.partial(kernel, micros, sections, token_total),...  159 us

profile of v3, /device:TPU:1, one launch (start us, length us, event | category | flops | bytes accessed | tf_op | source)
XLA Modules:
  0.0 163.0 jit_solution(17881377542152219656)
XLA Ops:
  0.6 158.8 %shard_map.77 = (f32[64,2048]{1,0:T(8,128)}, s32[1]{0:T(128)}) custom-call(bf16[256,2048]{1,0:T(8,128)(2,1)} %bitcast.7, bf16[256,2048]{1,0:T(8,128)(2,1)} %bitcast.8, bf16[64,2048]{1,0:T(8,128)(2,1)} %bitcast.10, f32[1,2048]{1,0:T(1,128)} %gain_ref.1, s32[512,2048]{1,0:T(8,128)} %bitcast.6, s32[16,2048]{1,0:T(8,128)} %bitcast.11), custom_call_target="tpu_custom_call" | custom-call | tf_op jit(solution)/shard_map/pallas_call | solution.py:501
  159.4 1.9 %copy.10 = f32[1,64,2048]{2,1,0:T(8,128)} copy(f32[1,64,2048]{2,1,0:T(8,128)} %bitcast.9) | data formatting | bytes 1048576

commit v4 on v3

--- a/solution.py
+++ b/solution.py
@@ -16,24 +16,24 @@
 BF = jnp.bfloat16
 F32 = jnp.float32
 SIDE = 4
+CHUNK = 1024
 BLOCKS = SIDE * SIDE
 
 
-def kernel(micros, sections, token_total, x_hbm, ct_hbm, weight_ref, gain_ref, pair_hbm, earlier_ref, out_ref, flip_ref,
+def kernel(sections, token_total, x_hbm, ct_hbm, weight_hbm, gain_hbm, pair_hbm, earlier_hbm, out_ref, flip_ref,
+           weight_ref, gain_ref, earlier_ref, own_pairs, first_sem,
            w, turned, packed, pair, wide_rows, decay, arriving, leaving, hidden, preact, slope, scale, mine, theirs,
            grad_pre, part, part_a, part_b, row_sum, row_a, row_b, flips,
-           local_sem, ag_send, ag_recv, mate_recv, in_send, in_recv, z_send, z_recv, mate_n, mate_g, mate_f, mate_send,
+           local_sem, ag_send, ag_recv, far_recv, mate_recv, in_send, in_recv, z_send, z_recv, mate_n, mate_g, mate_f, mate_send,
            a_recv, ab_recv, ra_recv, rb_recv, rs_send, flip_send, flip_recv):
     s = lax.axis_index("section")
     dp = lax.axis_index("dp")
     core, xx, yy = dp % 2, (dp // 2) % SIDE, dp // (2 * SIDE)
     last = sections - 1
-    rows_all, width = arriving.shape
-    rows = rows_all // micros
-    half_rows = rows_all // 2
+    micros, chunks, rows, chunk = arriving.shape
+    width = chunks * chunk
+    ahead = pl.ds(0, micros // 2), pl.ds(micros // 2, micros // 2)
     forward_core, backward_core = core == 1, core == 0
-    chunk = 512
-    chunks = width // chunk
     shard = weight_ref.shape[0]
     groups = shard // 4
     half_width = width // 2
@@ -51,20 +51,36 @@
         return pltpu.make_async_remote_copy(
             src_ref=src, dst_ref=dst, send_sem=send, recv_sem=recv, device_id={"dp": target}, device_id_type=MESH)
 
+    own_groups = pl.ds(pl.multiple_of(dp * groups, groups), groups)
+    first_copies = (
+        pltpu.make_async_copy(pair_hbm.at[own_groups], own_pairs, first_sem.at[0]),
+        pltpu.make_async_copy(weight_hbm, weight_ref, first_sem.at[1]),
+        pltpu.make_async_copy(earlier_hbm, earlier_ref, first_sem.at[2]),
+        pltpu.make_async_copy(gain_hbm, gain_ref, first_sem.at[3]),
+    )
+    for copy in first_copies:
+        copy.start()
     pair_copy = pltpu.make_async_copy(pair_hbm, pair, local_sem.at[0])
     pair_copy.start()
-    x_copy = pltpu.make_async_copy(x_hbm, arriving.at[pl.ds(0, half_rows)], local_sem.at[1])
-    ct_copy = pltpu.make_async_copy(ct_hbm, arriving.at[pl.ds(half_rows, half_rows)], local_sem.at[1])
-    x_mate = remote(x_hbm, arriving.at[pl.ds(half_rows, half_rows)], in_send.at[0], in_recv.at[0], mate)
-    ct_mate = remote(ct_hbm, arriving.at[pl.ds(0, half_rows)], in_send.at[0], in_recv.at[0], mate)
+    pieces = [pl.ds(c * chunk, chunk) for c in range(chunks)]
+    x_copies = [pltpu.make_async_copy(x_hbm.at[:, :, cols], arriving.at[ahead[0], c], local_sem.at[1 + c])
+                for c, cols in enumerate(pieces)]
+    ct_copies = [pltpu.make_async_copy(ct_hbm.at[:, :, cols], arriving.at[ahead[1], c], local_sem.at[1 + c])
+                 for c, cols in enumerate(pieces)]
+    x_mates = [remote(x_hbm.at[:, :, cols], arriving.at[ahead[1], c], in_send.at[c], in_recv.at[c], mate)
+               for c, cols in enumerate(pieces)]
+    ct_mates = [remote(ct_hbm.at[:, :, cols], arriving.at[ahead[0], c], in_send.at[c], in_recv.at[c], mate)
+                for c, cols in enumerate(pieces)]
 
     @pl.when((s == 0) & forward_core)
     def _():
-        x_copy.start()
+        for copy in x_copies:
+            copy.start()
 
     @pl.when((s == last) & backward_core)
     def _():
-        ct_copy.start()
+        for copy in ct_copies:
+            copy.start()
 
     barrier = pltpu.get_barrier_semaphore()
     for target in (*around, mate):
@@ -78,13 +94,13 @@
     def _():
         pl.semaphore_signal(barrier, inc=1, device_id={"section": s + 1}, device_id_type=MESH)
 
-    pair_copy.wait()
-    own_groups = pl.ds(pl.multiple_of(dp * groups, groups), groups)
     piece = 128
+    for copy in first_copies:
+        copy.wait()
     counted = jnp.zeros((8, 128), jnp.int32)
     for k in range(width // piece):
         cols = pl.ds(k * piece, piece)
-        p = pair[own_groups, cols]
+        p = own_pairs[:, cols]
         wide_rows[k] = weight_ref[:, cols].astype(F32)
         w0, w1, w2, w3 = (wide_rows[k, pl.ds(j, groups, stride=4), :] for j in range(4))
         lead = jnp.where(p < 3, w0, jnp.where(p == 5, w2, w1))
@@ -105,33 +121,38 @@
 
     @pl.when((s == 0) & backward_core)
     def _():
-        x_mate.start()
+        for copy in x_mates:
+            copy.start()
 
     @pl.when((s == last) & forward_core)
     def _():
-        ct_mate.start()
-
-    def send_half(b, h, d):
-        at = pl.ds(h * groups, groups)
-        remote(packed.at[2 * b + core, at], packed.at[2 * b + core, at], ag_send.at[d], ag_recv.at[b, h],
-               around[d]).start()
+        for copy in ct_mates:
+            copy.start()
+
+    def shard_copy(b, d, recv):
+        ref = packed.at[2 * b + core]
+        return remote(ref, ref, ag_send.at[d], recv, (*around, mate)[d])
+
+    def send_shard(b, d):
+        shard_copy(b, d, ag_recv.at[b]).start()
+
+    def wait_shard(b):
+        shard_copy(b, 0, ag_recv.at[b]).wait_recv()
+
+    def half_shard(b, h):
+        ref = packed.at[2 * b + core, pl.ds(h * groups, groups)]
+        return remote(ref, ref, ag_send.at[h], far_recv.at[h], around[h])
 
     def send_mate(b):
-        remote(packed.at[2 * b + core], packed.at[2 * b + core], ag_send.at[4], mate_recv.at[b], mate).start()
-
-    def wait_half(b, h):
-        at = pl.ds(h * groups, groups)
-        remote(packed.at[2 * b + core, at], packed.at[2 * b + core, at], ag_send.at[0], ag_recv.at[b, h],
-               mate).wait_recv()
+        shard_copy(b, 4, mate_recv.at[b]).start()
 
     def wait_mate(b):
         slot = 2 * b + (1 - core)
         remote(packed.at[slot], packed.at[slot], ag_send.at[4], mate_recv.at[b], mate).wait_recv()
 
     def spread(b):
-        for d in (2, 3):
-            send_half(b, 0, d)
-            send_half(b, 1, d)
+        send_shard(b, 2)
+        send_shard(b, 3)
         send_mate(b)
 
     def unpack(slot):
@@ -154,40 +175,44 @@
         return remote(flips.at[src], flips.at[dst], flip_send.at[dst - 1], flip_recv.at[dst - 1], target)
 
     own = chip(core, 0, 0)
-    for d in (0, 1):
-        send_half(own, 0, d)
-        send_half(own, 1, d)
+    send_shard(own, 0)
+    send_shard(own, 1)
     spread(own)
     flip_copy(0, 1, mate).start()
+    pair_copy.wait()
     unpack(dp)
     from_left, from_right, far = chip(core, 3, 0), chip(core, 1, 0), chip(core, 2, 0)
-    wait_half(from_left, 0)
-    send_half(from_left, 0, 0)
-    wait_half(from_left, 1)
+    wait_shard(from_left)
+    half_shard(from_left, 0).start()
     spread(from_left)
-    wait_half(from_right, 1)
-    send_half(from_right, 1, 1)
-    wait_half(from_right, 0)
+    wait_shard(from_right)
+    half_shard(from_right, 1).start()
     spread(from_right)
     flip_copy(0, 1, mate).wait_recv()
     flips[8] = flips[0] + flips[1]
     flip_copy(8, 2, right1).start()
     flip_copy(8, 3, left1).start()
     unpack(2 * from_left + core)
-    wait_half(far, 0)
-    wait_half(far, 1)
+    half_shard(far, 0).wait_recv()
+    half_shard(far, 1).wait_recv()
     spread(far)
 
     def near(i, carry):
         r1 = jnp.where(i == 0, 0, jnp.where(i == 1, 3, jnp.where(i == 2, 1, 2)))
         lower, upper = chip(core, r1, 3), chip(core, r1, 1)
-        wait_half(lower, 0)
-        send_half(lower, 0, 2)
-        wait_half(lower, 1)
+        wait_shard(lower)
+
+        @pl.when(i < 2)
+        def _():
+            send_shard(lower, 2)
+
         send_mate(lower)
-        wait_half(upper, 1)
-        send_half(upper, 1, 3)
-        wait_half(upper, 0)
+        wait_shard(upper)
+
+        @pl.when(i >= 2)
+        def _():
+            send_shard(upper, 3)
+
         send_mate(upper)
         other = chip(1 - core, r1, 0)
         wait_mate(other)
@@ -212,8 +237,7 @@
     def distant(i, carry):
         r1 = jnp.where(i == 0, 0, jnp.where(i == 1, 3, jnp.where(i == 2, 1, 2)))
         beyond = chip(core, r1, 2)
-        wait_half(beyond, 0)
-        wait_half(beyond, 1)
+        wait_shard(beyond)
         send_mate(beyond)
         lower, upper = chip(1 - core, r1, 3), chip(1 - core, r1, 1)
         wait_mate(lower)
@@ -252,11 +276,11 @@
             src_ref=leaving.at[where], dst_ref=arriving.at[where], send_sem=z_send.at[m], recv_sem=z_recv.at[m],
             device_id={"section": target}, device_id_type=MESH)
 
-    def forward_copy(m, where):
-        return z_copy(m, where, jnp.minimum(s + 1, last))
-
-    def backward_copy(m, where):
-        return z_copy(m, where, jnp.maximum(s - 1, 0))
+    def forward_copy(m, *where):
+        return z_copy(m, (m, *where), jnp.minimum(s + 1, last))
+
+    def backward_copy(m, *where):
+        return z_copy(m, (m, *where), jnp.maximum(s - 1, 0))
 
     def half_copy(m):
         return remote(theirs.at[tile_rows(m)], mine.at[tile_rows(m)], mate_send.at[0, m], mate_n.at[m], mate)
@@ -267,41 +291,57 @@
     def saved_copy(k, m):
         src = (arriving, slope, preact, scale)[k]
         dst = (hidden, slope, preact, scale)[k]
-        return remote(src.at[tile_rows(m)], dst.at[tile_rows(m)], mate_send.at[1 + k, m], mate_f.at[k, m], mate)
+        at = m if k == 0 else tile_rows(m)
+        return remote(src.at[at], dst.at[at], mate_send.at[1 + k, m], mate_f.at[k, m], mate)
 
     def forward(m, carry):
         at = tile_rows(m)
 
         @pl.when(s > 0)
         def _():
-            forward_copy(m, (at,)).wait_recv()
+            forward_copy(m).wait_recv()
 
         saved_copy(0, m).start()
-        values = arriving[at, :].astype(F32)
-        q = lax.rsqrt(jnp.sum(values * values, axis=-1, keepdims=True) * (1.0 / width) + epsilon)
+        gained, squares = [], 0.0
+        for c, cols in enumerate(pieces):
+            values = arriving[m, c].astype(F32)
+            gained.append((values * gain_ref[:, cols]).astype(BF))
+            squares += jnp.sum(values * values, axis=-1, keepdims=True)
+        gained = jnp.concatenate(gained, axis=1)
+        q = lax.rsqrt(squares * (1.0 / width) + epsilon)
         scale[at, :] = jnp.broadcast_to(q, (rows, 128))
-        normal = (values * q * gain_ref[...]).astype(BF)
-        for c in range(chunks):
-            cols = pl.ds(c * chunk, chunk)
-            p = jnp.dot(normal, w[:, cols], preferred_element_type=F32)
+        for c, cols in enumerate(pieces):
+            p = jnp.dot(gained, w[:, cols], preferred_element_type=F32) * q
             cdf = 0.5 * (1.0 + lax.erf(p * half_root))
-            leaving[at, cols] = (arriving[at, cols].astype(F32) + p * cdf).astype(BF)
+            leaving[m, c] = (arriving[m, c].astype(F32) + p * cdf).astype(BF)
 
             @pl.when(s < last)
             def _():
-                forward_copy(m, (at, cols)).start()
+                forward_copy(m, c).start()
 
             preact[at, cols] = p.astype(BF)
             slope[at, cols] = (cdf + p * (jnp.exp(-0.5 * p * p) * density_scale)).astype(BF)
         for k in (1, 2, 3):
             saved_copy(k, m).start()
+        return carry
+
+    def halves(m, carry):
+        at = tile_rows(m)
+        q = scale[at, :]
         low = lax.broadcasted_iota(jnp.int32, (rows, 128), 1) < 64
+
+        def scaled(start):
+            values = arriving[m, start // chunk, :, pl.ds(start % chunk, 128)].astype(F32)
+            return values * q * gain_ref[:, pl.ds(start, 128)]
+
         for k in range(width // 256):
-            first = arriving[at, pl.ds(256 * k, 128)].astype(F32) * q * gain_ref[:, pl.ds(256 * k, 128)]
-            second = arriving[at, pl.ds(256 * k + 128, 128)].astype(F32) * q * gain_ref[:, pl.ds(256 * k + 128, 128)]
+            first, second = scaled(256 * k), scaled(256 * k + 128)
             cols = pl.ds(128 * k, 128)
-            theirs[at, cols] = jnp.where(low, first, pltpu.roll(second, 64, 1)).astype(BF)
             mine[at, cols] = jnp.where(low, pltpu.roll(first, 64, 1), second).astype(BF)
+        for k in range(width // 256):
+            start = (k % 2) * 1024 + (k // 2) * 128
+            first, second = scaled(start), scaled(start + 512)
+            theirs[at, pl.ds(128 * k, 128)] = jnp.where(low, first, pltpu.roll(second, 64, 1)).astype(BF)
         half_copy(m).start()
         return carry
 
@@ -312,9 +352,11 @@
 
         @pl.when(s < last)
         def _():
-            backward_copy(m, (at,)).wait_recv()
-
-        gp = (arriving[at, :].astype(F32) * slope[at, :].astype(F32)).astype(BF)
+            backward_copy(m).wait_recv()
+
+        gp = jnp.concatenate(
+            [(arriving[m, c].astype(F32) * slope[at, cols].astype(F32)).astype(BF) for c, cols in enumerate(pieces)],
+            axis=1)
         grad_pre[at, :] = gp
         grad_copy(m).start()
 
@@ -323,12 +365,11 @@
             q = scale[at, 0:1]
             mean = jnp.sum(gp.astype(F32) * preact[at, :].astype(F32), axis=-1, keepdims=True) * (1.0 / width)
             pull = q * q * mean
-            for c in range(chunks):
-                cols = pl.ds(c * chunk, chunk)
+            for c, cols in enumerate(pieces):
                 a = jnp.dot(gp, turned[:, cols], preferred_element_type=F32)
                 a = a * gain_ref[:, cols]
-                leaving[at, cols] = (arriving[at, cols].astype(F32) + q * a - hidden[at, cols].astype(F32) * pull).astype(BF)
-                backward_copy(m, (at, cols)).start()
+                leaving[m, c] = (arriving[m, c].astype(F32) + q * a - hidden[m, c].astype(F32) * pull).astype(BF)
+                backward_copy(m, c).start()
         return carry
 
     def received_grad(m, carry):
@@ -343,10 +384,13 @@
     def _():
         @pl.when(s == 0)
         def _():
-            x_copy.wait()
-            x_mate.wait_recv()
+            for copy in x_copies:
+                copy.wait()
+            for copy in x_mates:
+                copy.wait_recv()
 
         lax.fori_loop(0, micros, forward, 0)
+        lax.fori_loop(0, micros, halves, 0)
         lax.fori_loop(0, micros, received_grad, 0)
 
     @pl.when(backward_core)
@@ -360,8 +404,10 @@
 
         @pl.when(s == last)
         def _():
-            ct_copy.wait()
-            ct_mate.wait_recv()
+            for copy in ct_copies:
+                copy.wait()
+            for copy in ct_mates:
+                copy.wait_recv()
 
         lax.fori_loop(0, micros, backward, 0)
         lax.fori_loop(0, micros, received_half, 0)
@@ -369,16 +415,17 @@
     flip_copy(9, 5, right2).wait_recv()
     flip_copy(5, 7, right2).start()
 
-    def terms(i, carry):
-        cols = pl.ds(pl.multiple_of(i * 256, 256), 256)
+    place1, place2 = jnp.where(core == 0, xx, yy), jnp.where(core == 0, yy, xx)
+
+    def block(r1, r2):
+        place = ((place1 + r1) % SIDE) * SIDE + (place2 + r2) % SIDE
+        return pl.ds(pl.multiple_of(place * shard, shard), shard)
+
+    def terms(i):
+        r1 = jnp.where(i == 0, 2, jnp.where(i == 1, 3, jnp.where(i == 2, 1, 0)))
+        cols = pl.ds(pl.multiple_of(((place1 + r1) % SIDE) * (SIDE * shard), SIDE * shard), SIDE * shard)
         part[cols, :] = lax.dot_general(
             mine[:, cols], grad_pre[...], (((0,), (0,)), ((), ())), preferred_element_type=F32).astype(BF)
-        return carry
-
-    lax.fori_loop(0, half_width // 256, terms, 0)
-
-    def block(r1, r2):
-        return pl.ds(pl.multiple_of(chip(core, r1, r2) * shard, shard), shard)
 
     def slot(r2, count=1):
         return pl.ds(r2 * shard, count * shard)
@@ -387,14 +434,28 @@
         return remote(part.at[block(src_r1, r2)], dst.at[dst_slot], rs_send.at[d], recv, around[d])
 
     toward_left, toward_right = (2, 1), (3, 0)
-    for r2 in toward_left:
-        first_ring(2, r2, 1, part_a, slot(r2), a_recv.at[r2]).start()
-    for r2 in toward_right:
-        first_ring(2, r2, 0, part_a, slot(r2), a_recv.at[r2]).start()
-    for r2 in toward_right:
-        first_ring(3, r2, 1, part_b, slot(r2), ab_recv.at[0, r2]).start()
-    for r2 in toward_left:
-        first_ring(1, r2, 0, part_b, slot(4 + r2), ab_recv.at[1, r2]).start()
+    def group(i, carry):
+        terms(i)
+
+        @pl.when(i == 0)
+        def _():
+            for k in range(2):
+                first_ring(2, toward_left[k], 1, part_a, slot(toward_left[k]), a_recv.at[toward_left[k]]).start()
+                first_ring(2, toward_right[k], 0, part_a, slot(toward_right[k]), a_recv.at[toward_right[k]]).start()
+
+        @pl.when(i == 1)
+        def _():
+            for r2 in toward_right:
+                first_ring(3, r2, 1, part_b, slot(r2), ab_recv.at[0, r2]).start()
+
+        @pl.when(i == 2)
+        def _():
+            for r2 in toward_left:
+                first_ring(1, r2, 0, part_b, slot(4 + r2), ab_recv.at[1, r2]).start()
+
+        return carry
+
+    lax.fori_loop(0, SIDE, group, 0)
     for k in range(2):
         for r2, r1, d, side in ((toward_left[k], 3, 1, 0), (toward_right[k], 1, 0, 1)):
             first_ring(2, r2, d, part_a, slot(r2), a_recv.at[r2]).wait_recv()
@@ -442,7 +503,7 @@
     def drain_forward(m, carry):
         @pl.when(s < last)
         def _():
-            forward_copy(m, (tile_rows(m),)).wait_send()
+            forward_copy(m).wait_send()
 
         half_copy(m).wait_send()
         for k in range(4):
@@ -452,7 +513,7 @@
     def drain_backward(m, carry):
         @pl.when(s > 0)
         def _():
-            backward_copy(m, (tile_rows(m),)).wait_send()
+            backward_copy(m).wait_send()
 
         grad_copy(m).wait_send()
         return carry
@@ -463,7 +524,8 @@
 
         @pl.when(s == last)
         def _():
-            ct_mate.wait_send()
+            for copy in ct_mates:
+                copy.wait_send()
 
     @pl.when(backward_core)
     def _():
@@ -471,7 +533,8 @@
 
         @pl.when(s == 0)
         def _():
-            x_mate.wait_send()
+            for copy in x_mates:
+                copy.wait_send()
 
     def sent(sem, count):
         ref = grad_pre.at[pl.ds(0, count)]
@@ -490,27 +553,32 @@
         flip_copy(0, dst, mate).wait_send()
 
 
-def step(x, ct, weight, gain, pair, earlier, sections, token_total, micros):
-    rows, width = x.shape
+def step(x, ct, weight, gain, pair, earlier, sections, token_total, chunk):
+    micros, tall, width = x.shape
+    micros, rows = 2 * micros, micros * tall
+    chunks = width // chunk
     shard = weight.shape[0]
     groups = shard // 4
     vmem = pl.BlockSpec(memory_space=pltpu.VMEM)
     hbm = pl.BlockSpec(memory_space=pl.ANY)
     act = pltpu.VMEM((2 * rows, width), BF)
+    stream = pltpu.VMEM((micros, chunks, tall, chunk), BF)
     dma = pltpu.SemaphoreType.DMA
     return pl.pallas_call(
-        functools.partial(kernel, micros, sections, token_total),
+        functools.partial(kernel, sections, token_total),
         out_shape=(jax.ShapeDtypeStruct((shard, width), F32), jax.ShapeDtypeStruct((1,), jnp.int32)),
-        in_specs=[hbm, hbm, vmem, vmem, hbm, vmem],
+        in_specs=[hbm] * 6,
         out_specs=(vmem, pl.BlockSpec(memory_space=pltpu.SMEM)),
         scratch_shapes=[
+            pltpu.VMEM((shard, width), BF), pltpu.VMEM((1, width), F32), pltpu.VMEM((groups, width), jnp.int32),
+            pltpu.VMEM((groups, width), jnp.int32), dma((4,)),
             pltpu.VMEM((width, width), BF),
             pltpu.VMEM((width, width), BF),
             pltpu.VMEM((2 * BLOCKS, 2 * groups, width), BF),
             pltpu.VMEM(pair.shape, jnp.int32),
             pltpu.VMEM((width // 128, shard, 128), F32),
             pltpu.VMEM((width // 128, shard, 128), F32),
-            act, act, act, act, act, pltpu.VMEM((2 * rows, 128), F32),
+            stream, stream, stream, act, act, pltpu.VMEM((2 * rows, 128), F32),
             pltpu.VMEM((2 * rows, width // 2), BF),
             pltpu.VMEM((2 * rows, width // 2), BF),
             pltpu.VMEM((2 * rows, width), BF),
@@ -521,7 +589,7 @@
             pltpu.VMEM((shard, width), BF),
             pltpu.VMEM((2 * shard, width), BF),
             pltpu.VMEM((10, 8, 128), jnp.int32),
-            dma((2,)), dma((5,)), dma((BLOCKS, 2)), dma((BLOCKS,)), dma((1,)), dma((1,)),
+            dma((1 + chunks,)), dma((5,)), dma((BLOCKS,)), dma((2,)), dma((BLOCKS,)), dma((chunks,)), dma((chunks,)),
             dma((micros,)), dma((micros,)), dma((micros,)), dma((micros,)), dma((4, micros)), dma((5, micros)),
             dma((SIDE,)), dma((2, SIDE)), dma((2,)), dma((2, 2)), dma((4,)), dma((7,)), dma((7,)),
         ],
@@ -533,9 +601,11 @@
 def body(activations, cotangent, weight, norm_gain, pair_mask, earlier_mask):
     micro_count, row_count, model_width = activations.shape
     tokens = micro_count * row_count
+    tall = 32
     gradient, flip_sum = step(
-        activations.reshape(tokens, model_width), cotangent.reshape(tokens, model_width), weight[0], norm_gain,
-        pair_mask[0], earlier_mask[0], lax.axis_size("section"), tokens * lax.axis_size("dp"), 16)
+        activations.reshape(tokens // tall, tall, model_width), cotangent.reshape(tokens // tall, tall, model_width),
+        weight[0], norm_gain, pair_mask[0], earlier_mask[0], lax.axis_size("section"),
+        tokens * lax.axis_size("dp"), CHUNK)
     return (gradient[None], flip_sum)
 
 

time: 163 us -> 155 us (0.951)
  Pallas kernels: 159 us -> 151 us
    pallas_call x1, Pallas kernels: 159 us -> 151 us  [step(): pl.pallas_call(functools.partial(kernel, sections, token_total), out_shap...]
where the time goes in v4:
time: 155 us
  Pallas kernels  151 us (97%)
  between operations  2.34 us (2%)
  local copies, waits for them, and re-layouts  1.87 us (1%)
    pallas_call x1, Pallas kernels, step(): pl.pallas_call(functools.partial(kernel, sections, token_total), out_shap...  151 us

profile of v4, /device:TPU:1, one launch (start us, length us, event | category | flops | bytes accessed | tf_op | source)
XLA Modules:
  0.0 154.9 jit_solution(513704842641224298)
XLA Ops:
  0.6 150.6 %shard_map.77 = (f32[64,2048]{1,0:T(8,128)}, s32[1]{0:T(128)}) custom-call(bf16[8,32,2048]{2,1,0:T(8,128)(2,1)} %bitcast.7, bf16[8,32,2048]{2,1,0:T(8,128)(2,1)} %bitcast.8, bf16[64,2048]{1,0:T(8,128)(2,1)} %bitcast.10, f32[1,2048]{1,0:T(1,128)} %gain_hbm.1, s32[512,2048]{1,0:T(8,128)} %bitcast.6, s32[16,2048]{1,0:T(8,128)} %bitcast.11), custom_call_target="tpu_custom_call" | custom-call | tf_op jit(solution)/shard_map/pallas_call | solution.py:567
  151.3 1.9 %copy.10 = f32[1,64,2048]{2,1,0:T(8,128)} copy(f32[1,64,2048]{2,1,0:T(8,128)} %bitcast.9) | data formatting | bytes 1048576

commit v5 on v4

--- a/solution.py
+++ b/solution.py
@@ -17,12 +17,13 @@
 F32 = jnp.float32
 SIDE = 4
 CHUNK = 1024
+TAIL = 3
 BLOCKS = SIDE * SIDE
 
 
 def kernel(sections, token_total, x_hbm, ct_hbm, weight_hbm, gain_hbm, pair_hbm, earlier_hbm, out_ref, flip_ref,
            weight_ref, gain_ref, earlier_ref, own_pairs, first_sem,
-           w, turned, packed, pair, wide_rows, decay, arriving, leaving, hidden, preact, slope, scale, mine, theirs,
+           w, turned, packed, pair, wide_rows, decay, arriving, leaving, hidden, tail_out, t_send, t_recv, preact, slope, scale, mine, theirs,
            grad_pre, part, part_a, part_b, row_sum, row_a, row_b, flips,
            local_sem, ag_send, ag_recv, far_recv, mate_recv, in_send, in_recv, z_send, z_recv, mate_n, mate_g, mate_f, mate_send,
            a_recv, ab_recv, ra_recv, rb_recv, rs_send, flip_send, flip_recv):
@@ -32,6 +33,7 @@
     last = sections - 1
     micros, chunks, rows, chunk = arriving.shape
     width = chunks * chunk
+    early = micros - TAIL
     ahead = pl.ds(0, micros // 2), pl.ds(micros // 2, micros // 2)
     forward_core, backward_core = core == 1, core == 0
     shard = weight_ref.shape[0]
@@ -71,6 +73,9 @@
                for c, cols in enumerate(pieces)]
     ct_mates = [remote(ct_hbm.at[:, :, cols], arriving.at[ahead[0], c], in_send.at[c], in_recv.at[c], mate)
                 for c, cols in enumerate(pieces)]
+
+    tail_mates = [remote(ct_hbm.at[pl.ds(micros // 2 - TAIL, TAIL), :, cols], hidden.at[pl.ds(early, TAIL), c],
+                         in_send.at[c], in_recv.at[c], mate) for c, cols in enumerate(pieces)]
 
     @pl.when((s == 0) & forward_core)
     def _():
@@ -129,6 +134,11 @@
         for copy in ct_mates:
             copy.start()
 
+    @pl.when((s == last) & backward_core)
+    def _():
+        for copy in tail_mates:
+            copy.start()
+
     def shard_copy(b, d, recv):
         ref = packed.at[2 * b + core]
         return remote(ref, ref, ag_send.at[d], recv, (*around, mate)[d])
@@ -271,22 +281,27 @@
     def tile_rows(m):
         return pl.ds(pl.multiple_of(m * rows, rows), rows)
 
-    def z_copy(m, where, target):
+    def z_copy(src, dst, send, recv, target):
         return pltpu.make_async_remote_copy(
-            src_ref=leaving.at[where], dst_ref=arriving.at[where], send_sem=z_send.at[m], recv_sem=z_recv.at[m],
-            device_id={"section": target}, device_id_type=MESH)
+            src_ref=src, dst_ref=dst, send_sem=send, recv_sem=recv, device_id={"section": target}, device_id_type=MESH)
 
     def forward_copy(m, *where):
-        return z_copy(m, (m, *where), jnp.minimum(s + 1, last))
+        at = (m, *where)
+        return z_copy(leaving.at[at], arriving.at[at], z_send.at[m], z_recv.at[m], jnp.minimum(s + 1, last))
 
     def backward_copy(m, *where):
-        return z_copy(m, (m, *where), jnp.maximum(s - 1, 0))
+        at = (m, *where)
+        return z_copy(leaving.at[at], arriving.at[at], z_send.at[m], z_recv.at[m], jnp.maximum(s - 1, 0))
+
+    def tail_copy(m, *where):
+        return z_copy(tail_out.at[(m - early, *where)], hidden.at[(m, *where)], t_send.at[m - early],
+                      t_recv.at[m - early], jnp.maximum(s - 1, 0))
 
     def half_copy(m):
         return remote(theirs.at[tile_rows(m)], mine.at[tile_rows(m)], mate_send.at[0, m], mate_n.at[m], mate)
 
     def grad_copy(m):
-        return remote(grad_pre.at[tile_rows(m)], grad_pre.at[tile_rows(m)], mate_send.at[0, m], mate_g.at[m], mate)
+        return remote(grad_pre.at[tile_rows(m)], grad_pre.at[tile_rows(m)], mate_send.at[5, m], mate_g.at[m], mate)
 
     def saved_copy(k, m):
         src = (arriving, slope, preact, scale)[k]
@@ -301,7 +316,6 @@
         def _():
             forward_copy(m).wait_recv()
 
-        saved_copy(0, m).start()
         gained, squares = [], 0.0
         for c, cols in enumerate(pieces):
             values = arriving[m, c].astype(F32)
@@ -321,8 +335,12 @@
 
             preact[at, cols] = p.astype(BF)
             slope[at, cols] = (cdf + p * (jnp.exp(-0.5 * p * p) * density_scale)).astype(BF)
-        for k in (1, 2, 3):
-            saved_copy(k, m).start()
+
+        @pl.when(m < early)
+        def _():
+            for k in (1, 2, 0, 3):
+                saved_copy(k, m).start()
+
         return carry
 
     def halves(m, carry):
@@ -345,20 +363,17 @@
         half_copy(m).start()
         return carry
 
-    def backward(m, carry):
+    def backward_rows(m, upstream, inputs, result, place, z):
         at = tile_rows(m)
-        for k in (0, 1, 2, 3):
-            saved_copy(k, m).wait_recv()
 
         @pl.when(s < last)
         def _():
-            backward_copy(m).wait_recv()
+            z(m).wait_recv()
 
         gp = jnp.concatenate(
-            [(arriving[m, c].astype(F32) * slope[at, cols].astype(F32)).astype(BF) for c, cols in enumerate(pieces)],
+            [(upstream[m, c].astype(F32) * slope[at, cols].astype(F32)).astype(BF) for c, cols in enumerate(pieces)],
             axis=1)
         grad_pre[at, :] = gp
-        grad_copy(m).start()
 
         @pl.when(s > 0)
         def _():
@@ -368,8 +383,24 @@
             for c, cols in enumerate(pieces):
                 a = jnp.dot(gp, turned[:, cols], preferred_element_type=F32)
                 a = a * gain_ref[:, cols]
-                leaving[m, c] = (arriving[m, c].astype(F32) + q * a - hidden[m, c].astype(F32) * pull).astype(BF)
-                backward_copy(m, c).start()
+                result[place, c] = (upstream[m, c].astype(F32) + q * a - inputs[m, c].astype(F32) * pull).astype(BF)
+                z(m, c).start()
+
+        grad_copy(m).start()
+
+    def backward(m, carry):
+        for k in (0, 1, 2, 3):
+            saved_copy(k, m).wait_recv()
+        backward_rows(m, arriving, hidden, leaving, m, backward_copy)
+        return carry
+
+    def backward_tail(m, carry):
+        backward_rows(m, hidden, arriving, tail_out, m - early, tail_copy)
+        return carry
+
+    def turn(i, carry):
+        at = pl.ds(pl.multiple_of(i * 128, 128), 128)
+        turned[:, at] = w[at, :].T
         return carry
 
     def received_grad(m, carry):
@@ -389,17 +420,35 @@
             for copy in x_mates:
                 copy.wait_recv()
 
+        @pl.when(s > 1)
+        def _():
+            lax.fori_loop(0, width // 128, turn, 0)
+
         lax.fori_loop(0, micros, forward, 0)
-        lax.fori_loop(0, micros, halves, 0)
-        lax.fori_loop(0, micros, received_grad, 0)
+
+        @pl.when(s == 1)
+        def _():
+            lax.fori_loop(0, width // 128, turn, 0)
+
+        @pl.when(s < 4)
+        def _():
+            lax.fori_loop(0, micros, halves, 0)
+
+        @pl.when(s == last)
+        def _():
+            for copy in tail_mates:
+                copy.wait_recv()
+
+        lax.fori_loop(early, micros, backward_tail, 0)
+
+        @pl.when(s >= 4)
+        def _():
+            lax.fori_loop(0, micros, halves, 0)
+
+        lax.fori_loop(0, early, received_grad, 0)
 
     @pl.when(backward_core)
     def _():
-        def turn(i, carry):
-            at = pl.ds(pl.multiple_of(i * 128, 128), 128)
-            turned[:, at] = w[at, :].T
-            return carry
-
         lax.fori_loop(0, width // 128, turn, 0)
 
         @pl.when(s == last)
@@ -409,8 +458,9 @@
             for copy in ct_mates:
                 copy.wait_recv()
 
-        lax.fori_loop(0, micros, backward, 0)
+        lax.fori_loop(0, early, backward, 0)
         lax.fori_loop(0, micros, received_half, 0)
+        lax.fori_loop(early, micros, received_grad, 0)
 
     flip_copy(9, 5, right2).wait_recv()
     flip_copy(5, 7, right2).start()
@@ -506,10 +556,21 @@
             forward_copy(m).wait_send()
 
         half_copy(m).wait_send()
+        return carry
+
+    def drain_saved(m, carry):
         for k in range(4):
             saved_copy(k, m).wait_send()
         return carry
 
+    def drain_tail(m, carry):
+        @pl.when(s > 0)
+        def _():
+            tail_copy(m).wait_send()
+
+        grad_copy(m).wait_send()
+        return carry
+
     def drain_backward(m, carry):
         @pl.when(s > 0)
         def _():
@@ -521,6 +582,8 @@
     @pl.when(forward_core)
     def _():
         lax.fori_loop(0, micros, drain_forward, 0)
+        lax.fori_loop(0, early, drain_saved, 0)
+        lax.fori_loop(early, micros, drain_tail, 0)
 
         @pl.when(s == last)
         def _():
@@ -529,7 +592,12 @@
 
     @pl.when(backward_core)
     def _():
-        lax.fori_loop(0, micros, drain_backward, 0)
+        lax.fori_loop(0, early, drain_backward, 0)
+
+        @pl.when(s == last)
+        def _():
+            for copy in tail_mates:
+                copy.wait_send()
 
         @pl.when(s == 0)
         def _():
@@ -578,7 +646,7 @@
             pltpu.VMEM(pair.shape, jnp.int32),
             pltpu.VMEM((width // 128, shard, 128), F32),
             pltpu.VMEM((width // 128, shard, 128), F32),
-            stream, stream, stream, act, act, pltpu.VMEM((2 * rows, 128), F32),
+            stream, stream, stream, pltpu.VMEM((TAIL, chunks, tall, chunk), BF), dma((TAIL,)), dma((TAIL,)), act, act, pltpu.VMEM((2 * rows, 128), F32),
             pltpu.VMEM((2 * rows, width // 2), BF),
             pltpu.VMEM((2 * rows, width // 2), BF),
             pltpu.VMEM((2 * rows, width), BF),
@@ -590,7 +658,7 @@
             pltpu.VMEM((2 * shard, width), BF),
             pltpu.VMEM((10, 8, 128), jnp.int32),
             dma((1 + chunks,)), dma((5,)), dma((BLOCKS,)), dma((2,)), dma((BLOCKS,)), dma((chunks,)), dma((chunks,)),
-            dma((micros,)), dma((micros,)), dma((micros,)), dma((micros,)), dma((4, micros)), dma((5, micros)),
+            dma((micros,)), dma((micros,)), dma((micros,)), dma((micros,)), dma((4, micros)), dma((6, micros)),
             dma((SIDE,)), dma((2, SIDE)), dma((2,)), dma((2, 2)), dma((4,)), dma((7,)), dma((7,)),
         ],
         compiler_params=pltpu.CompilerParams(

time: 155 us -> 156 us (level)
  no operation moved by 1% of the time
where the time goes in v5:
time: 156 us; the launch traced here: 155 us
  Pallas kernels  150 us (96%)
  between operations  2.34 us (2%)
  local copies, waits for them, and re-layouts  1.87 us (1%)
    pallas_call x1, Pallas kernels, step(): pl.pallas_call(functools.partial(kernel, sections, token_total), out_shap...  150 us

profile of v5, /device:TPU:1, one launch (start us, length us, event | category | flops | bytes accessed | tf_op | source)
XLA Modules:
  0.0 154.7 jit_solution(7372516658125483153)
XLA Ops:
  0.6 150.5 %shard_map.77 = (f32[64,2048]{1,0:T(8,128)}, s32[1]{0:T(128)}) custom-call(bf16[8,32,2048]{2,1,0:T(8,128)(2,1)} %bitcast.7, bf16[8,32,2048]{2,1,0:T(8,128)(2,1)} %bitcast.8, bf16[64,2048]{1,0:T(8,128)(2,1)} %bitcast.10, f32[1,2048]{1,0:T(1,128)} %gain_hbm.1, s32[512,2048]{1,0:T(8,128)} %bitcast.6, s32[16,2048]{1,0:T(8,128)} %bitcast.11), custom_call_target="tpu_custom_call" | custom-call | tf_op jit(solution)/shard_map/pallas_call | solution.py:635
  151.1 1.9 %copy.10 = f32[1,64,2048]{2,1,0:T(8,128)} copy(f32[1,64,2048]{2,1,0:T(8,128)} %bitcast.9) | data formatting | bytes 1048576

commit v6 on v4

--- a/solution.py
+++ b/solution.py
@@ -22,7 +22,7 @@
 
 def kernel(sections, token_total, x_hbm, ct_hbm, weight_hbm, gain_hbm, pair_hbm, earlier_hbm, out_ref, flip_ref,
            weight_ref, gain_ref, earlier_ref, own_pairs, first_sem,
-           w, turned, packed, pair, wide_rows, decay, arriving, leaving, hidden, preact, slope, scale, mine, theirs,
+           partial, w, turned, packed, pair, wide_rows, decay, arriving, leaving, hidden, preact, slope, scale, mine, theirs,
            grad_pre, part, part_a, part_b, row_sum, row_a, row_b, flips,
            local_sem, ag_send, ag_recv, far_recv, mate_recv, in_send, in_recv, z_send, z_recv, mate_n, mate_g, mate_f, mate_send,
            a_recv, ab_recv, ra_recv, rb_recv, rs_send, flip_send, flip_recv):
@@ -271,16 +271,16 @@
     def tile_rows(m):
         return pl.ds(pl.multiple_of(m * rows, rows), rows)
 
-    def z_copy(m, where, target):
+    def z_copy(m, c, target):
         return pltpu.make_async_remote_copy(
-            src_ref=leaving.at[where], dst_ref=arriving.at[where], send_sem=z_send.at[m], recv_sem=z_recv.at[m],
+            src_ref=leaving.at[m, c], dst_ref=arriving.at[m, c], send_sem=z_send.at[m, c], recv_sem=z_recv.at[m, c],
             device_id={"section": target}, device_id_type=MESH)
 
-    def forward_copy(m, *where):
-        return z_copy(m, (m, *where), jnp.minimum(s + 1, last))
-
-    def backward_copy(m, *where):
-        return z_copy(m, (m, *where), jnp.maximum(s - 1, 0))
+    def forward_copy(m, c):
+        return z_copy(m, c, jnp.minimum(s + 1, last))
+
+    def backward_copy(m, c):
+        return z_copy(m, c, jnp.maximum(s - 1, 0))
 
     def half_copy(m):
         return remote(theirs.at[tile_rows(m)], mine.at[tile_rows(m)], mate_send.at[0, m], mate_n.at[m], mate)
@@ -296,22 +296,23 @@
 
     def forward(m, carry):
         at = tile_rows(m)
-
-        @pl.when(s > 0)
-        def _():
-            forward_copy(m).wait_recv()
-
-        saved_copy(0, m).start()
-        gained, squares = [], 0.0
-        for c, cols in enumerate(pieces):
-            values = arriving[m, c].astype(F32)
-            gained.append((values * gain_ref[:, cols]).astype(BF))
+        squares = 0.0
+        for k, deep in enumerate(pieces):
+            @pl.when(s > 0)
+            def _():
+                forward_copy(m, k).wait_recv()
+
+            values = arriving[m, k].astype(F32)
+            gained = (values * gain_ref[:, deep]).astype(BF)
             squares += jnp.sum(values * values, axis=-1, keepdims=True)
-        gained = jnp.concatenate(gained, axis=1)
+            if k < chunks - 1:
+                for cols in pieces:
+                    term = jnp.dot(gained, w[deep, cols], preferred_element_type=F32)
+                    partial[:, cols] = term if k == 0 else partial[:, cols] + term
         q = lax.rsqrt(squares * (1.0 / width) + epsilon)
         scale[at, :] = jnp.broadcast_to(q, (rows, 128))
         for c, cols in enumerate(pieces):
-            p = jnp.dot(gained, w[:, cols], preferred_element_type=F32) * q
+            p = (partial[:, cols] + jnp.dot(gained, w[deep, cols], preferred_element_type=F32)) * q
             cdf = 0.5 * (1.0 + lax.erf(p * half_root))
             leaving[m, c] = (arriving[m, c].astype(F32) + p * cdf).astype(BF)
 
@@ -321,7 +322,7 @@
 
             preact[at, cols] = p.astype(BF)
             slope[at, cols] = (cdf + p * (jnp.exp(-0.5 * p * p) * density_scale)).astype(BF)
-        for k in (1, 2, 3):
+        for k in (1, 2, 0, 3):
             saved_copy(k, m).start()
         return carry
 
@@ -349,27 +350,33 @@
         at = tile_rows(m)
         for k in (0, 1, 2, 3):
             saved_copy(k, m).wait_recv()
-
-        @pl.when(s < last)
-        def _():
-            backward_copy(m).wait_recv()
-
-        gp = jnp.concatenate(
-            [(arriving[m, c].astype(F32) * slope[at, cols].astype(F32)).astype(BF) for c, cols in enumerate(pieces)],
-            axis=1)
-        grad_pre[at, :] = gp
-        grad_copy(m).start()
+        inner = 0.0
+        for k, deep in enumerate(pieces):
+            @pl.when(s < last)
+            def _():
+                backward_copy(m, k).wait_recv()
+
+            gp = (arriving[m, k].astype(F32) * slope[at, deep].astype(F32)).astype(BF)
+            grad_pre[at, deep] = gp
+            inner += jnp.sum(gp.astype(F32) * preact[at, deep].astype(F32), axis=-1, keepdims=True)
+            if k < chunks - 1:
+                @pl.when(s > 0)
+                def _():
+                    for cols in pieces:
+                        term = jnp.dot(gp, turned[deep, cols], preferred_element_type=F32)
+                        partial[:, cols] = term if k == 0 else partial[:, cols] + term
 
         @pl.when(s > 0)
         def _():
             q = scale[at, 0:1]
-            mean = jnp.sum(gp.astype(F32) * preact[at, :].astype(F32), axis=-1, keepdims=True) * (1.0 / width)
-            pull = q * q * mean
+            pull = q * q * (inner * (1.0 / width))
             for c, cols in enumerate(pieces):
-                a = jnp.dot(gp, turned[:, cols], preferred_element_type=F32)
+                a = partial[:, cols] + jnp.dot(gp, turned[deep, cols], preferred_element_type=F32)
                 a = a * gain_ref[:, cols]
                 leaving[m, c] = (arriving[m, c].astype(F32) + q * a - hidden[m, c].astype(F32) * pull).astype(BF)
                 backward_copy(m, c).start()
+
+        grad_copy(m).start()
         return carry
 
     def received_grad(m, carry):
@@ -456,6 +463,54 @@
         return carry
 
     lax.fori_loop(0, SIDE, group, 0)
+    def drain_forward(m, carry):
+        @pl.when(s < last)
+        def _():
+            for c in range(chunks):
+                forward_copy(m, c).wait_send()
+
+        half_copy(m).wait_send()
+        for k in range(4):
+            saved_copy(k, m).wait_send()
+        return carry
+
+    def drain_backward(m, carry):
+        @pl.when(s > 0)
+        def _():
+            for c in range(chunks):
+                backward_copy(m, c).wait_send()
+
+        grad_copy(m).wait_send()
+        return carry
+
+    @pl.when(forward_core)
+    def _():
+        lax.fori_loop(0, micros, drain_forward, 0)
+
+        @pl.when(s == last)
+        def _():
+            for copy in ct_mates:
+                copy.wait_send()
+
+    @pl.when(backward_core)
+    def _():
+        lax.fori_loop(0, micros, drain_backward, 0)
+
+        @pl.when(s == 0)
+        def _():
+            for copy in x_mates:
+                copy.wait_send()
+
+    def sent(sem, count):
+        ref = grad_pre.at[pl.ds(0, count)]
+        remote(ref, ref, sem, flip_recv.at[0], mate).wait_send()
+
+    for d in (0, 1):
+        sent(ag_send.at[d], 3 * groups)
+    for d in (2, 3):
+        sent(ag_send.at[d], 12 * groups)
+    sent(ag_send.at[4], 2 * BLOCKS * groups)
+
     for k in range(2):
         for r2, r1, d, side in ((toward_left[k], 3, 1, 0), (toward_right[k], 1, 0, 1)):
             first_ring(2, r2, d, part_a, slot(r2), a_recv.at[r2]).wait_recv()
@@ -500,51 +555,6 @@
         total = row_sum[slot(0), cols].astype(F32) + row_b[slot(0), cols].astype(F32) + row_b[slot(1), cols].astype(F32)
         out_ref[:, cols] = total * (1.0 / math.sqrt(token_total)) + decay[k]
 
-    def drain_forward(m, carry):
-        @pl.when(s < last)
-        def _():
-            forward_copy(m).wait_send()
-
-        half_copy(m).wait_send()
-        for k in range(4):
-            saved_copy(k, m).wait_send()
-        return carry
-
-    def drain_backward(m, carry):
-        @pl.when(s > 0)
-        def _():
-            backward_copy(m).wait_send()
-
-        grad_copy(m).wait_send()
-        return carry
-
-    @pl.when(forward_core)
-    def _():
-        lax.fori_loop(0, micros, drain_forward, 0)
-
-        @pl.when(s == last)
-        def _():
-            for copy in ct_mates:
-                copy.wait_send()
-
-    @pl.when(backward_core)
-    def _():
-        lax.fori_loop(0, micros, drain_backward, 0)
-
-        @pl.when(s == 0)
-        def _():
-            for copy in x_mates:
-                copy.wait_send()
-
-    def sent(sem, count):
-        ref = grad_pre.at[pl.ds(0, count)]
-        remote(ref, ref, sem, flip_recv.at[0], mate).wait_send()
-
-    for d in (0, 1):
-        sent(ag_send.at[d], 3 * groups)
-    for d in (2, 3):
-        sent(ag_send.at[d], 12 * groups)
-    sent(ag_send.at[4], 2 * BLOCKS * groups)
     for d in (0, 1):
         sent(rs_send.at[d], 6 * shard)
     for d in (2, 3):
@@ -572,6 +582,7 @@
         scratch_shapes=[
             pltpu.VMEM((shard, width), BF), pltpu.VMEM((1, width), F32), pltpu.VMEM((groups, width), jnp.int32),
             pltpu.VMEM((groups, width), jnp.int32), dma((4,)),
+            pltpu.VMEM((tall, width), F32),
             pltpu.VMEM((width, width), BF),
             pltpu.VMEM((width, width), BF),
             pltpu.VMEM((2 * BLOCKS, 2 * groups, width), BF),
@@ -590,7 +601,7 @@
             pltpu.VMEM((2 * shard, width), BF),
             pltpu.VMEM((10, 8, 128), jnp.int32),
             dma((1 + chunks,)), dma((5,)), dma((BLOCKS,)), dma((2,)), dma((BLOCKS,)), dma((chunks,)), dma((chunks,)),
-            dma((micros,)), dma((micros,)), dma((micros,)), dma((micros,)), dma((4, micros)), dma((5, micros)),
+            dma((micros, chunks)), dma((micros, chunks)), dma((micros,)), dma((micros,)), dma((4, micros)), dma((5, micros)),
             dma((SIDE,)), dma((2, SIDE)), dma((2,)), dma((2, 2)), dma((4,)), dma((7,)), dma((7,)),
         ],
         compiler_params=pltpu.CompilerParams(

time: 155 us -> 154 us (level)
  no operation moved by 1% of the time
where the time goes in v6:
time: 154 us
  Pallas kernels  150 us (97%)
  between operations  2.34 us (2%)
  local copies, waits for them, and re-layouts  1.87 us (1%)
    pallas_call x1, Pallas kernels, step(): pl.pallas_call(functools.partial(kernel, sections, token_total), out_shap...  150 us

profile of v6, /device:TPU:1, one launch (start us, length us, event | category | flops | bytes accessed | tf_op | source)
XLA Modules:
  0.0 154.2 jit_solution(17603858717047116321)
XLA Ops:
  0.6 150.0 %shard_map.77 = (f32[64,2048]{1,0:T(8,128)}, s32[1]{0:T(128)}) custom-call(bf16[8,32,2048]{2,1,0:T(8,128)(2,1)} %bitcast.7, bf16[8,32,2048]{2,1,0:T(8,128)(2,1)} %bitcast.8, bf16[64,2048]{1,0:T(8,128)(2,1)} %bitcast.10, f32[1,2048]{1,0:T(1,128)} %gain_hbm.1, s32[512,2048]{1,0:T(8,128)} %bitcast.6, s32[16,2048]{1,0:T(8,128)} %bitcast.11), custom_call_target="tpu_custom_call" | custom-call | tf_op jit(solution)/shard_map/pallas_call | solution.py:577
  150.6 1.9 %copy.10 = f32[1,64,2048]{2,1,0:T(8,128)} copy(f32[1,64,2048]{2,1,0:T(8,128)} %bitcast.9) | data formatting | bytes 1048576

commit v7 on v6

--- a/solution.py
+++ b/solution.py
@@ -309,6 +309,10 @@
                 for cols in pieces:
                     term = jnp.dot(gained, w[deep, cols], preferred_element_type=F32)
                     partial[:, cols] = term if k == 0 else partial[:, cols] + term
+        @pl.when(s == last)
+        def _():
+            saved_copy(0, m).start()
+
         q = lax.rsqrt(squares * (1.0 / width) + epsilon)
         scale[at, :] = jnp.broadcast_to(q, (rows, 128))
         for c, cols in enumerate(pieces):
@@ -322,8 +326,13 @@
 
             preact[at, cols] = p.astype(BF)
             slope[at, cols] = (cdf + p * (jnp.exp(-0.5 * p * p) * density_scale)).astype(BF)
-        for k in (1, 2, 0, 3):
+        for k in (1, 2, 3):
             saved_copy(k, m).start()
+
+        @pl.when(s < last)
+        def _():
+            saved_copy(0, m).start()
+
         return carry
 
     def halves(m, carry):
@@ -348,7 +357,7 @@
 
     def backward(m, carry):
         at = tile_rows(m)
-        for k in (0, 1, 2, 3):
+        for k in (1, 2):
             saved_copy(k, m).wait_recv()
         inner = 0.0
         for k, deep in enumerate(pieces):
@@ -365,6 +374,9 @@
                     for cols in pieces:
                         term = jnp.dot(gp, turned[deep, cols], preferred_element_type=F32)
                         partial[:, cols] = term if k == 0 else partial[:, cols] + term
+
+        for k in (0, 3):
+            saved_copy(k, m).wait_recv()
 
         @pl.when(s > 0)
         def _():

time: 154 us -> 154 us (level)
  no operation moved by 1% of the time
where the time goes in v7:
time: 154 us
  Pallas kernels  150 us (97%)
  between operations  2.34 us (2%)
  local copies, waits for them, and re-layouts  1.87 us (1%)
    pallas_call x1, Pallas kernels, step(): pl.pallas_call(functools.partial(kernel, sections, token_total), out_shap...  150 us

profile of v7, /device:TPU:1, one launch (start us, length us, event | category | flops | bytes accessed | tf_op | source)
XLA Modules:
  0.0 154.0 jit_solution(1688107318359717419)
XLA Ops:
  0.6 149.8 %shard_map.77 = (f32[64,2048]{1,0:T(8,128)}, s32[1]{0:T(128)}) custom-call(bf16[8,32,2048]{2,1,0:T(8,128)(2,1)} %bitcast.7, bf16[8,32,2048]{2,1,0:T(8,128)(2,1)} %bitcast.8, bf16[64,2048]{1,0:T(8,128)(2,1)} %bitcast.10, f32[1,2048]{1,0:T(1,128)} %gain_hbm.1, s32[512,2048]{1,0:T(8,128)} %bitcast.6, s32[16,2048]{1,0:T(8,128)} %bitcast.11), custom_call_target="tpu_custom_call" | custom-call | tf_op jit(solution)/shard_map/pallas_call | solution.py:589
  150.4 1.9 %copy.10 = f32[1,64,2048]{2,1,0:T(8,128)} copy(f32[1,64,2048]{2,1,0:T(8,128)} %bitcast.9) | data formatting | bytes 1048576
